TPU v7x, 32 devices: a whole 2x2x4 slice. The times are simulated.
32 devices in a mesh: dp: 16 (over z, y, x), tensor: 2 (over core).
Axes of the slice: x: 2, y: 2, z: 4, core: 2. Of those that a mesh axis runs over, the one named last changes fastest.
Arguments:
- inputs: bfloat16 [4, 8192, 768], P(None, ('dp', 'tensor')), may hold values from -6 to 6
- lengths: int32 [4, 16], P(None, 'dp'), may hold values from 128 to 512, as said below
- bounds: int32 [4, 16], P(None, 'dp'), may hold values from 32 to 384, as said below
- query_matrix: bfloat16 [768, 768], P('dp', 'tensor'), may hold values from -0.21875 to 0.21875
- key_matrix: bfloat16 [768, 768], P('dp', 'tensor'), may hold values from -0.21875 to 0.21875
- value_matrix: bfloat16 [768, 768], P('dp', 'tensor'), may hold values from -0.21875 to 0.21875
- query_value_bias: float32 [2, 768], P(None, 'tensor'), may hold values from -3 to 3
- adapter_down_weight: bfloat16 [2, 768, 8], P(None, 'dp'), may hold values from -0.21875 to 0.21875
- adapter_up_weight: bfloat16 [2, 8, 768], P(None, None, 'tensor'), may hold values from -1 to 1
- attention_output_weight: bfloat16 [768, 768], P('tensor', 'dp'), may hold values from -1.75 to 1.75
- feedforward_input_weight: bfloat16 [768, 3072], P('dp', 'tensor'), may hold values from -0.21875 to 0.21875
- feedforward_input_bias: float32 [3072], P('tensor'), may hold values from -3 to 3
- feedforward_output_weight: bfloat16 [3072, 768], P('tensor', 'dp'), may hold values from -0.109375 to 0.109375
- output_bias: float32 [2, 768], replicated, may hold values from -3 to 3
- layernorm_scale: float32 [2, 768], replicated, may hold values from 0.5 to 1.5
- layernorm_bias: float32 [2, 768], replicated, may hold values from -2 to 2
- output_gradient: bfloat16 [4, 8192, 768], P(None, ('dp', 'tensor')), may hold values from -6 to 6
Outputs:
- outputs: bfloat16 [4, 8192, 768], P(None, ('dp', 'tensor'))
- input_grad: float32 [4, 8192, 768], P(None, ('dp', 'tensor'))
- lora_up_grad: float32 [2, 8, 768], P(None, None, 'tensor')
Inputs may be any that keep to these rules, and one draw needn't show every extreme that they name: Item i of micro-batch m has live positions 0 to lengths[m, i] - 1 of its 512; the others are padding. An item's first segment is positions 0 to bounds - 1, its second bounds to 511; bounds lies between lengths // 4 and 3 * lengths // 4.
All inputs are finite; a program needn't handle non-finite values.
Results may differ from a plain program's by a relative error of at most 0.015.
The roundings to bfloat16 on the way count: a program that leaves them out, or rounds other values in their place, can miss the bound.
Values may be sent and summed in bfloat16 or wider, within the bound.
No kernel may reach another device: no remote copies, remote signals or barrier semaphores. Data moves between devices by JAX's collectives and lax.ppermute only.
A program may use at most 192 MiB of HBM per device.

v0:
```python
import jax
import jax.numpy as jnp
from jax import lax
from jax.sharding import PartitionSpec as P

HEAD_DIM = 64
UPDATE_RANK = 8
SLOT = 512


adapter_scale = 2.0
masked_value = -1000000000.0
norm_eps = 1e-05
highest_precision = lax.Precision.HIGHEST


def layer_norm(value_rows, gain, shift):
    centre = value_rows - jnp.mean(value_rows, axis=-1, keepdims=True)
    spread = jnp.mean(centre * centre, axis=-1, keepdims=True)
    return centre * lax.rsqrt(spread + norm_eps) * gain + shift


def exact_gelu(value_rows):
    return jax.nn.gelu(value_rows, approximate=False)


def item_mask(length, bound):
    places = jnp.arange(SLOT)
    segment = places >= bound
    return (places < length)[None, :] & (segment[:, None] == segment[None, :])


def split_heads(input_array):
    return input_array.reshape(input_array.shape[0], input_array.shape[1] // HEAD_DIM, HEAD_DIM)


def item_scores(query_heads, key_heads, length, bound):
    scores = (
        jnp.einsum("qhd,khd->hqk", query_heads, key_heads, preferred_element_type=jnp.float32)
        * 0.125
    )
    return jnp.where(item_mask(length, bound)[None], scores, masked_value)


def attend_forward(pieces):
    query_rows, keys, value_rows, length, bound = pieces
    query_heads = split_heads(query_rows)
    value_heads = split_heads(value_rows)
    scores = item_scores(query_heads, split_heads(keys), length, bound)
    peak = jnp.max(scores, axis=-1, keepdims=True)
    totals = jnp.log(jnp.sum(jnp.exp(scores - peak), axis=-1, keepdims=True)) + peak
    soft_weights = jnp.exp(scores - totals).astype(jnp.bfloat16)
    mixed = jnp.einsum(
        "hqk,khd->qhd", soft_weights, value_heads, preferred_element_type=jnp.float32
    )
    return (mixed.reshape(SLOT, query_rows.shape[1]).astype(jnp.bfloat16), totals)


def attend_backward(pieces):
    query_rows, keys, value_rows, grad_mixed, totals, length, bound = pieces
    query_heads = split_heads(query_rows)
    key_heads = split_heads(keys)
    grad_heads = split_heads(grad_mixed)
    scores = item_scores(query_heads, key_heads, length, bound)
    probs = jnp.exp(scores - totals)
    value_gradient = jnp.einsum(
        "hqk,qhd->khd", probs.astype(jnp.bfloat16), grad_heads, preferred_element_type=jnp.float32
    )
    grad_probs = jnp.einsum(
        "qhd,khd->hqk", grad_heads, split_heads(value_rows), preferred_element_type=jnp.float32
    )
    inner = jnp.sum(probs * grad_probs, axis=-1, keepdims=True)
    grad_scores = (probs * (grad_probs - inner)).astype(jnp.bfloat16)
    query_gradient = (
        jnp.einsum("hqk,khd->qhd", grad_scores, key_heads, preferred_element_type=jnp.float32)
        * 0.125
    )
    key_gradient = (
        jnp.einsum("hqk,qhd->khd", grad_scores, query_heads, preferred_element_type=jnp.float32)
        * 0.125
    )
    width = query_rows.shape[1]
    return (
        query_gradient.reshape(SLOT, width).astype(jnp.bfloat16),
        key_gradient.reshape(SLOT, width).astype(jnp.bfloat16),
        value_gradient.reshape(SLOT, width).astype(jnp.bfloat16),
    )


def contract_trailing(left, right):
    return lax.dot_general(
        left, right, (((1,), (1,)), ((), ())), preferred_element_type=jnp.float32
    )


def project_row_batch(
    input_rows,
    query_projected,
    key_projected,
    value_projected,
    down_projected,
    query_value_bias,
    adapter_up_weight,
):
    up_weight_float = adapter_up_weight.astype(jnp.float32)
    lowrank_update = jnp.einsum(
        "td,zdr->ztr", input_rows, down_projected, preferred_element_type=jnp.float32
    )
    query_rows = (
        jnp.dot(input_rows, query_projected, preferred_element_type=jnp.float32)
        + query_value_bias[0]
        + adapter_scale
        * jnp.dot(lowrank_update[0], up_weight_float[0], precision=highest_precision)
    ).astype(jnp.bfloat16)
    keys = jnp.dot(input_rows, key_projected, preferred_element_type=jnp.float32).astype(
        jnp.bfloat16
    )
    value_rows = (
        jnp.dot(input_rows, value_projected, preferred_element_type=jnp.float32)
        + query_value_bias[1]
        + adapter_scale
        * jnp.dot(lowrank_update[1], up_weight_float[1], precision=highest_precision)
    ).astype(jnp.bfloat16)
    return (lowrank_update, query_rows, keys, value_rows)


def adapter_components(lowrank_update, query_gradient, value_gradient):
    first_dims = (((0,), (0,)), ((), ()))
    return adapter_scale * jnp.stack(
        [
            lax.dot_general(
                lowrank_update[0],
                query_gradient.astype(jnp.float32),
                first_dims,
                precision=highest_precision,
            ),
            lax.dot_general(
                lowrank_update[1],
                value_gradient.astype(jnp.float32),
                first_dims,
                precision=highest_precision,
            ),
        ]
    )


def input_terms_all(
    query_gradient,
    key_gradient,
    value_gradient,
    query_projected,
    key_projected,
    value_projected,
    down_projected,
    adapter_up_weight,
):
    query_lowrank_gradient = adapter_scale * contract_trailing(query_gradient, adapter_up_weight[0])
    value_lowrank_gradient = adapter_scale * contract_trailing(value_gradient, adapter_up_weight[1])
    down_float = down_projected.astype(jnp.float32)
    total = contract_trailing(query_gradient, query_projected)
    total = total + contract_trailing(key_gradient, key_projected)
    total = total + contract_trailing(value_gradient, value_projected)
    total = total + lax.dot_general(
        query_lowrank_gradient, down_float[0], (((1,), (1,)), ((), ())), precision=highest_precision
    )
    total = total + lax.dot_general(
        value_lowrank_gradient, down_float[1], (((1,), (1,)), ((), ())), precision=highest_precision
    )
    return total


def forward_pass(rows_local, item_lengths, item_bounds, gathered, parameters):
    (
        query_projected,
        key_projected,
        value_projected,
        down_projected,
        out_full,
        ffn_in_full,
        ffn_out_full,
    ) = gathered
    (
        query_value_bias,
        adapter_up_weight,
        feedforward_input_bias,
        output_bias,
        layernorm_scale,
        layernorm_bias,
    ) = parameters
    group_items = item_lengths.shape[0]
    row_groups = lax.all_gather(rows_local, "tensor", axis=0, tiled=True)
    lowrank_update, query_rows, keys, value_rows = project_row_batch(
        row_groups,
        query_projected,
        key_projected,
        value_projected,
        down_projected,
        query_value_bias,
        adapter_up_weight,
    )
    width = query_rows.shape[1]
    item_shape = (group_items, SLOT, width)
    mixed, totals = lax.map(
        attend_forward,
        (
            query_rows.reshape(item_shape),
            keys.reshape(item_shape),
            value_rows.reshape(item_shape),
            item_lengths,
            item_bounds,
        ),
    )
    mixed_rows = mixed.reshape(group_items * SLOT, width)
    attended = lax.psum_scatter(
        jnp.dot(mixed_rows, out_full, preferred_element_type=jnp.float32),
        "tensor",
        scatter_dimension=0,
        tiled=True,
    )
    hidden_sum = rows_local.astype(jnp.float32) + attended + output_bias[0]
    normed = layer_norm(hidden_sum, layernorm_scale[0], layernorm_bias[0])
    pre_act = (
        jnp.dot(
            lax.all_gather(normed.astype(jnp.bfloat16), "tensor", axis=0, tiled=True),
            ffn_in_full,
            preferred_element_type=jnp.float32,
        )
        + feedforward_input_bias
    )
    activated = exact_gelu(pre_act).astype(jnp.bfloat16)
    ffn_total = (
        normed
        + lax.psum_scatter(
            jnp.dot(activated, ffn_out_full, preferred_element_type=jnp.float32),
            "tensor",
            scatter_dimension=0,
            tiled=True,
        )
        + output_bias[1]
    )
    result = layer_norm(ffn_total, layernorm_scale[1], layernorm_bias[1]).astype(jnp.bfloat16)
    kept = (lowrank_update, query_rows, keys, value_rows, totals, hidden_sum, pre_act, ffn_total)
    return (result, kept)


def layer_backward(grad_out, item_lengths, item_bounds, gathered, parameters, kept):
    (
        query_projected,
        key_projected,
        value_projected,
        down_projected,
        out_full,
        ffn_in_full,
        ffn_out_full,
    ) = gathered
    (
        query_value_bias,
        adapter_up_weight,
        feedforward_input_bias,
        output_bias,
        layernorm_scale,
        layernorm_bias,
    ) = parameters
    lowrank_update, query_rows, keys, value_rows, totals, hidden_sum, pre_act, ffn_total = kept
    group_items = item_lengths.shape[0]
    outer_pull = jax.vjp(
        lambda field: layer_norm(field, layernorm_scale[1], layernorm_bias[1]), ffn_total
    )[1]
    grad_sum = outer_pull(grad_out.astype(jnp.float32))[0]
    grad_act = contract_trailing(
        lax.all_gather(grad_sum.astype(jnp.bfloat16), "tensor", axis=0, tiled=True), ffn_out_full
    )
    gelu_pull = jax.vjp(exact_gelu, pre_act)[1]
    grad_pre = gelu_pull(grad_act)[0].astype(jnp.bfloat16)
    grad_normed = grad_sum + lax.psum_scatter(
        contract_trailing(grad_pre, ffn_in_full), "tensor", scatter_dimension=0, tiled=True
    )
    inner_pull = jax.vjp(
        lambda field: layer_norm(field, layernorm_scale[0], layernorm_bias[0]), hidden_sum
    )[1]
    grad_hidden = inner_pull(grad_normed)[0]
    grad_mixed = contract_trailing(
        lax.all_gather(grad_hidden.astype(jnp.bfloat16), "tensor", axis=0, tiled=True), out_full
    ).astype(jnp.bfloat16)
    width = query_rows.shape[1]
    item_shape = (group_items, SLOT, width)
    query_gradient, key_gradient, value_gradient = lax.map(
        attend_backward,
        (
            query_rows.reshape(item_shape),
            keys.reshape(item_shape),
            value_rows.reshape(item_shape),
            grad_mixed.reshape(item_shape),
            totals,
            item_lengths,
            item_bounds,
        ),
    )
    query_gradient = query_gradient.reshape(group_items * SLOT, width)
    key_gradient = key_gradient.reshape(group_items * SLOT, width)
    value_gradient = value_gradient.reshape(group_items * SLOT, width)
    adapter_portion = adapter_components(lowrank_update, query_gradient, value_gradient)
    row_gradient = grad_hidden + lax.psum_scatter(
        input_terms_all(
            query_gradient,
            key_gradient,
            value_gradient,
            query_projected,
            key_projected,
            value_projected,
            down_projected,
            adapter_up_weight,
        ).astype(jnp.bfloat16),
        "tensor",
        scatter_dimension=0,
        tiled=True,
    ).astype(jnp.float32)
    return (row_gradient, adapter_portion)


def local(
    inputs,
    lengths,
    bounds,
    query_matrix,
    key_matrix,
    value_matrix,
    query_value_bias,
    adapter_down_weight,
    adapter_up_weight,
    attention_output_weight,
    feedforward_input_weight,
    feedforward_input_bias,
    feedforward_output_weight,
    output_bias,
    layernorm_scale,
    layernorm_bias,
    output_gradient,
):
    micro_count = inputs.shape[0]
    parameters = (
        query_value_bias,
        adapter_up_weight,
        feedforward_input_bias,
        output_bias,
        layernorm_scale,
        layernorm_bias,
    )
    result_list = []
    gradient_tree = []
    adapter_combined = jnp.zeros((2, UPDATE_RANK, adapter_up_weight.shape[2]), jnp.float32)
    for batch_index in range(micro_count):
        forward_set = (
            lax.all_gather(query_matrix, "dp", axis=0, tiled=True),
            lax.all_gather(key_matrix, "dp", axis=0, tiled=True),
            lax.all_gather(value_matrix, "dp", axis=0, tiled=True),
            lax.all_gather(adapter_down_weight, "dp", axis=1, tiled=True),
            lax.all_gather(attention_output_weight, "dp", axis=1, tiled=True),
            lax.all_gather(feedforward_input_weight, "dp", axis=0, tiled=True),
            lax.all_gather(feedforward_output_weight, "dp", axis=1, tiled=True),
        )
        result, kept = forward_pass(
            inputs[batch_index], lengths[batch_index], bounds[batch_index], forward_set, parameters
        )
        backward_set = (
            lax.all_gather(query_matrix, "dp", axis=0, tiled=True),
            lax.all_gather(key_matrix, "dp", axis=0, tiled=True),
            lax.all_gather(value_matrix, "dp", axis=0, tiled=True),
            lax.all_gather(adapter_down_weight, "dp", axis=1, tiled=True),
            lax.all_gather(attention_output_weight, "dp", axis=1, tiled=True),
            lax.all_gather(feedforward_input_weight, "dp", axis=0, tiled=True),
            lax.all_gather(feedforward_output_weight, "dp", axis=1, tiled=True),
        )
        row_gradient, adapter_portion = layer_backward(
            output_gradient[batch_index],
            lengths[batch_index],
            bounds[batch_index],
            backward_set,
            parameters,
            kept,
        )
        adapter_combined = adapter_combined + lax.psum(adapter_portion, "dp")
        result_list.append(result)
        gradient_tree.append(row_gradient)
    return (jnp.stack(result_list), jnp.stack(gradient_tree), adapter_combined)


def solution(mesh):
    return jax.shard_map(
        local,
        mesh=mesh,
        in_specs=(
            P(None, ("dp", "tensor"), None),
            P(None, "dp"),
            P(None, "dp"),
            P("dp", "tensor"),
            P("dp", "tensor"),
            P("dp", "tensor"),
            P(None, "tensor"),
            P(None, "dp", None),
            P(None, None, "tensor"),
            P("tensor", "dp"),
            P("dp", "tensor"),
            P("tensor"),
            P("tensor", "dp"),
            P(),
            P(),
            P(),
            P(None, ("dp", "tensor"), None),
        ),
        out_specs=(
            P(None, ("dp", "tensor"), None),
            P(None, ("dp", "tensor"), None),
            P(None, None, "tensor"),
        ),
        check_vma=False,
    )
```

profile of v0, /device:TPU:0, one launch (start us, length us, event | category | flops | bytes accessed | tf_op | source)
XLA Modules:
  0.0 771.9 jit_solution(13941130316083166364)
XLA Ops:
  12.5 44.5 %all_gather.48 = bf16[2,768,8]{2,0,1:T(2,128)(2,1)S(1)} all-gather(bf16[2,48,8]{2,0,1:T(2,128)(2,1)S(1)} %copy.57), channel_id=1, replica_groups=mesh['dp'=16,'tensor'=2] {'dp'}, dimensions={1}, use_global_device_ids=true | all-gather | bytes 26112 | tf_op jit(solution)/shard_map/all_gather | solution.py:357
  57.3 39.2 %all_gather.49 = bf16[768,384]{1,0:T(8,128)(2,1)S(1)} all-gather(bf16[48,384]{1,0:T(8,128)(2,1)} %param.20), channel_id=1, replica_groups=mesh['dp'=16,'tensor'=2] {'dp'}, dimensions={0}, use_global_device_ids=true | all-gather | bytes 626688 | tf_op jit(solution)/shard_map/all_gather | solution.py:354
  96.5 41.1 %all_gather.50 = bf16[768,384]{1,0:T(8,128)(2,1)S(1)} all-gather(bf16[48,384]{1,0:T(8,128)(2,1)} %param.21), channel_id=1, replica_groups=mesh['dp'=16,'tensor'=2] {'dp'}, dimensions={0}, use_global_device_ids=true | all-gather | bytes 626688 | tf_op jit(solution)/shard_map/all_gather | solution.py:355
  137.5 39.3 %all_gather.47 = bf16[768,384]{1,0:T(8,128)(2,1)S(1)} all-gather(bf16[48,384]{1,0:T(8,128)(2,1)} %param.22), channel_id=1, replica_groups=mesh['dp'=16,'tensor'=2] {'dp'}, dimensions={0}, use_global_device_ids=true | all-gather | bytes 626688 | tf_op jit(solution)/shard_map/all_gather | solution.py:356
  176.8 40.8 %all_gather.51 = bf16[384,768]{0,1:T(8,128)(2,1)S(1)} all-gather(bf16[384,48]{0,1:T(8,128)(2,1)} %param.26), channel_id=1, replica_groups=mesh['dp'=16,'tensor'=2] {'dp'}, dimensions={1}, use_global_device_ids=true | all-gather | bytes 626688 | tf_op jit(solution)/shard_map/all_gather | solution.py:358
  289.6 47.5 %all-gather.7.cloned.1.call-done = bf16[768,1536]{1,0:T(8,128)(2,1)} async-done(((bf16[48,1536]{1,0:T(8,128)(2,1)}), bf16[768,1536]{1,0:T(8,128)(2,1)}) %all-gather.7.cloned.1.call-update) | async-done | bytes 2359312 | tf_op jit(solution)/shard_map/all_gather | solution.py:359
  337.1 10.4 %fusion.11 = (f32[512,1536]{1,0:T(8,128)}, f32[512,1536]{1,0:T(8,128)}) fusion(f32[1536]{0:T(1024)S(1)} %copy-done.198, bf16[512,768]{1,0:T(8,128)(2,1)S(1)} %all_gather.60, bf16[768,1536]{1,0:T(8,128)(2,1)} %all-gather.7.cloned.1.call-done), kind=kOutput, calls=%fused_computation.39 | convolution fusion | flops 1257504768 | bytes 9443328 | tf_op jit(solution)/shard_map/dot_general | solution.py:223
  347.5 52.7 %all-gather.9.cloned.1.call-done = bf16[1536,768]{0,1:T(8,128)(2,1)} async-done(((bf16[1536,48]{0,1:T(8,128)(2,1)}), bf16[1536,768]{0,1:T(8,128)(2,1)}) %all-gather.9.cloned.1.call-update) | async-done | bytes 2359312 | tf_op jit(solution)/shard_map/all_gather | solution.py:360
  400.2 6.1 fusion.35
  408.8 9.7 %fusion.10 = (f32[512,1536]{1,0:T(8,128)S(1)}, f32[512,1536]{1,0:T(8,128)S(1)}) fusion(f32[1536]{0:T(1024)} %param.28, bf16[512,768]{1,0:T(8,128)(2,1)S(1)} %all_gather.58, bf16[768,1536]{1,0:T(8,128)(2,1)} %all-gather.7.cloned.1.call-done), kind=kOutput, calls=%fused_computation.38 | convolution fusion | flops 1257504768 | bytes 9443328 | tf_op jit(solution)/shard_map/dot_general | solution.py:223
  426.2 9.5 %fusion.9 = (f32[512,1536]{1,0:T(8,128)S(1)}, f32[512,1536]{1,0:T(8,128)S(1)}) fusion(f32[1536]{0:T(1024)} %param.28, bf16[512,768]{1,0:T(8,128)(2,1)S(1)} %all_gather.56, bf16[768,1536]{1,0:T(8,128)(2,1)} %all-gather.7.cloned.1.call-done), kind=kOutput, calls=%fused_computation.37 | convolution fusion | flops 1257504768 | bytes 9443328 | tf_op jit(solution)/shard_map/dot_general | solution.py:223
  443.0 5.7 reduce-scatter.23.cloned.1.call-done
  455.6 8.1 %fusion.8 = (f32[512,1536]{1,0:T(8,128)S(1)}, f32[512,1536]{1,0:T(8,128)S(1)}) fusion(f32[1536]{0:T(1024)S(1)} %copy-done.199, bf16[512,768]{1,0:T(8,128)(2,1)S(1)} %all_gather.52, bf16[768,1536]{1,0:T(8,128)(2,1)S(1)} %copy-done.197), kind=kOutput, calls=%fused_computation.36 | convolution fusion | flops 1257504768 | bytes 9443328 | tf_op jit(solution)/shard_map/dot_general | solution.py:223
  469.0 10.4 %reduce-scatter.19.cloned.1.call-done = f32[256,768]{1,0:T(8,128)} async-done(((f32[512,768]{1,0:T(8,128)}), f32[256,768]{1,0:T(8,128)}) %reduce-scatter.19.cloned.1.call-update) | async-done | bytes 786448 | tf_op jit(solution)/shard_map/reduce_scatter | solution.py:233
  489.5 7.8 %fusion.43 = f32[512,768]{1,0:T(8,128)} fusion(bf16[768,1536]{1,0:T(8,128)(2,1)} %all-gather.7.cloned.1.call-done, f32[512,1536]{1,0:T(8,128)} %get-tuple-element.339, f32[512,1536]{1,0:T(8,128)} %get-tuple-element.340, bf16[512,768]{1,0:T(8,128)(2,1)} %all_gather.67, bf16[1536,768]{0,1:T(8,128)(2,1)S(1)} %copy-done.4), kind=kOutput, calls=%fused_computation.117 | convolution fusion | flops 2426929152 | bytes 13369344 | tf_op jit(solution)/shard_map/dot_general | solution.py:91
  507.4 7.8 %fusion.42 = f32[512,768]{1,0:T(8,128)} fusion(bf16[768,1536]{1,0:T(8,128)(2,1)} %all-gather.7.cloned.1.call-done, f32[512,1536]{1,0:T(8,128)} %copy-done.82, f32[512,1536]{1,0:T(8,128)} %copy-done.83, bf16[512,768]{1,0:T(8,128)(2,1)} %all_gather.65, bf16[1536,768]{0,1:T(8,128)(2,1)S(1)} %copy-done.4), kind=kOutput, calls=%fused_computation.116 | convolution fusion | flops 2426929152 | bytes 13369344 | tf_op jit(solution)/shard_map/dot_general | solution.py:91
  519.3 8.1 %fusion.40 = f32[512,768]{1,0:T(8,128)} fusion(bf16[768,1536]{1,0:T(8,128)(2,1)} %all-gather.7.cloned.1.call-done, f32[512,1536]{1,0:T(8,128)} %copy-done.84, f32[512,1536]{1,0:T(8,128)} %copy-done.85, bf16[512,768]{1,0:T(8,128)(2,1)} %all_gather.61, bf16[1536,768]{0,1:T(8,128)(2,1)S(1)} %copy-done.4), kind=kOutput, calls=%fused_computation.114 | convolution fusion | flops 2426929152 | bytes 13369344 | tf_op jit(solution)/shard_map/dot_general | solution.py:91
  531.3 7.8 %fusion.41 = f32[512,768]{1,0:T(8,128)} fusion(bf16[768,1536]{1,0:T(8,128)(2,1)} %all-gather.7.cloned.1.call-done, f32[512,1536]{1,0:T(8,128)} %copy-done.80, f32[512,1536]{1,0:T(8,128)} %copy-done.81, bf16[512,768]{1,0:T(8,128)(2,1)} %all_gather.63, bf16[1536,768]{0,1:T(8,128)(2,1)S(1)} %copy-done.4), kind=kOutput, calls=%fused_computation.115 | convolution fusion | flops 2426929152 | bytes 13369344 | tf_op jit(solution)/shard_map/dot_general | solution.py:91
  545.2 6.2 reduce-scatter.37.cloned.1.call-done
  594.2 6.5 multiply_convert_fusion.3
  613.4 5.6 multiply_reduce_fusion
  622.7 6.7 multiply_convert_fusion.2
  631.1 4.9 multiply_convert_fusion.1
  677.0 77.1 %psum.34 = f32[2,8,384]{2,1,0:T(8,128)} all-reduce(f32[2,8,384]{2,1,0:T(8,128)S(1)} %fusion.110), channel_id=1, replica_groups=mesh['dp'=16,'tensor'=2] {'dp'}, use_global_device_ids=true, to_apply=%region_60.61 | all-reduce | flops 6144 | bytes 49152 | tf_op jit(solution)/shard_map/psum | solution.py:382
  (678 shorter events, 249.7 us)
Async XLA Ops:
  8.0 270.3 %reduce-scatter.21.cloned.1.call-start = ((), (), s32[]{:S(2)}) async-start(), calls=%async_computation.20 | async-start | bytes 2359296 | tf_op jit(solution)/shard_map/reduce_scatter | solution.py:214
  57.3 207.7 %copy-start.88 = (bf16[2,768,8]{1,2,0:T(8,128)(2,1)}, bf16[2,768,8]{1,2,0:T(8,128)(2,1)S(1)}, u32[]{:S(2)}) copy-start(bf16[2,768,8]{1,2,0:T(8,128)(2,1)S(1)} %copy.58) | copy-start | bytes 73732
  57.3 160.3 %copy-start.53 = (bf16[4,256,768]{2,1,0:T(8,128)(2,1)S(1)}, bf16[4,256,768]{2,1,0:T(8,128)(2,1)}, u32[]{:S(2)}) copy-start(bf16[4,256,768]{2,1,0:T(8,128)(2,1)} %param.17) | copy-start | bytes 4718596
  96.5 168.8 %copy-start.19 = (bf16[768,384]{1,0:T(8,128)(2,1)}, bf16[768,384]{1,0:T(8,128)(2,1)S(1)}, u32[]{:S(2)}) copy-start(bf16[768,384]{1,0:T(8,128)(2,1)S(1)} %all_gather.49) | copy-start | bytes 1769476
  137.5 130.3 %copy-start.14 = (bf16[768,384]{1,0:T(8,128)(2,1)}, bf16[768,384]{1,0:T(8,128)(2,1)S(1)}, u32[]{:S(2)}) copy-start(bf16[768,384]{1,0:T(8,128)(2,1)S(1)} %all_gather.50) | copy-start | bytes 1769476
  176.8 94.1 %copy-start.22 = (bf16[768,384]{1,0:T(8,128)(2,1)}, bf16[768,384]{1,0:T(8,128)(2,1)S(1)}, u32[]{:S(2)}) copy-start(bf16[768,384]{1,0:T(8,128)(2,1)S(1)} %all_gather.47) | copy-start | bytes 1769476
  232.9 45.5 %reduce-scatter.17.cloned.1.call-start = ((), (), s32[]{:S(2)}) async-start(), calls=%async_computation.16 | async-start | bytes 2359296 | tf_op jit(solution)/shard_map/reduce_scatter | solution.py:214
  247.4 31.0 %reduce-scatter.29.cloned.1.call-start = ((), (), s32[]{:S(2)}) async-start(), calls=%async_computation.24 | async-start | bytes 2359296 | tf_op jit(solution)/shard_map/reduce_scatter | solution.py:214
  261.5 19.5 %reduce-scatter.25.cloned.1.call-start = ((), (), s32[]{:S(2)}) async-start(), calls=%async_computation.22 | async-start | bytes 2359296 | tf_op jit(solution)/shard_map/reduce_scatter | solution.py:214
  275.9 61.2 %all-gather.7.cloned.1.call-start = ((), (), s32[]{:S(2)}) async-start(), calls=%async_computation.17 | async-start | bytes 2506752 | tf_op jit(solution)/shard_map/all_gather | solution.py:359
  276.4 123.8 %all-gather.9.cloned.1.call-start = ((), (), s32[]{:S(2)}) async-start(), calls=%async_computation.18 | async-start | bytes 2506752 | tf_op jit(solution)/shard_map/all_gather | solution.py:360
  277.0 165.9 %reduce-scatter.31.cloned.1.call-start = ((), (), s32[]{:S(2)}) async-start(), calls=%async_computation.25 | async-start | bytes 2359296 | tf_op jit(solution)/shard_map/reduce_scatter | solution.py:233
  406.4 36.6 %reduce-scatter.27.cloned.1.call-start = ((), (), s32[]{:S(2)}) async-start(), calls=%async_computation.23 | async-start | bytes 2359296 | tf_op jit(solution)/shard_map/reduce_scatter | solution.py:233
  423.8 24.9 %reduce-scatter.23.cloned.1.call-start = ((), (), s32[]{:S(2)}) async-start(), calls=%async_computation.21 | async-start | bytes 2359296 | tf_op jit(solution)/shard_map/reduce_scatter | solution.py:233
  441.1 38.3 %reduce-scatter.19.cloned.1.call-start = ((), (), s32[]{:S(2)}) async-start(), calls=%async_computation.19 | async-start | bytes 2359296 | tf_op jit(solution)/shard_map/reduce_scatter | solution.py:233
  468.9 73.0 %reduce-scatter.45.cloned.1.call-start = ((), (), s32[]{:S(2)}) async-start(), calls=%async_computation.32 | async-start | bytes 2359296 | tf_op jit(solution)/shard_map/reduce_scatter | solution.py:275
  497.4 44.6 %reduce-scatter.41.cloned.1.call-start = ((), (), s32[]{:S(2)}) async-start(), calls=%async_computation.30 | async-start | bytes 2359296 | tf_op jit(solution)/shard_map/reduce_scatter | solution.py:275
  515.3 26.7 %reduce-scatter.33.cloned.1.call-start = ((), (), s32[]{:S(2)}) async-start(), calls=%async_computation.26 | async-start | bytes 2359296 | tf_op jit(solution)/shard_map/reduce_scatter | solution.py:275
  527.4 23.9 %reduce-scatter.37.cloned.1.call-start = ((), (), s32[]{:S(2)}) async-start(), calls=%async_computation.28 | async-start | bytes 2359296 | tf_op jit(solution)/shard_map/reduce_scatter | solution.py:275
  539.1 215.0 %reduce-scatter.35.cloned.1.call-start = ((), (), s32[]{:S(2)}) async-start(), calls=%async_computation.27 | async-start | bytes 1179648 | tf_op jit(solution)/shard_map/reduce_scatter | solution.py:303
  622.6 133.5 %reduce-scatter.39.cloned.1.call-start = ((), (), s32[]{:S(2)}) async-start(), calls=%async_computation.29 | async-start | bytes 1179648 | tf_op jit(solution)/shard_map/reduce_scatter | solution.py:303
  650.5 107.8 %reduce-scatter.43.cloned.1.call-start = ((), (), s32[]{:S(2)}) async-start(), calls=%async_computation.31 | async-start | bytes 1179648 | tf_op jit(solution)/shard_map/reduce_scatter | solution.py:303
  660.2 100.1 %reduce-scatter.47.cloned.1.call-start = ((), (), s32[]{:S(2)}) async-start(), calls=%async_computation.33 | async-start | bytes 1179648 | tf_op jit(solution)/shard_map/reduce_scatter | solution.py:303
  669.7 88.5 %copy-start.35 = (f32[256,768]{1,0:T(8,128)S(1)}, f32[256,768]{1,0:T(8,128)}, u32[]{:S(2)}) copy-start(f32[256,768]{1,0:T(8,128)} %copy-done.34) | copy-start | bytes 2359300
  (208 other events, 1464.1 us)
Sparse Core Ops, SparseCore 0:
  233.0 5.0 reduce-scatter.20
  247.5 5.1 reduce-scatter.16
  261.6 5.0 reduce-scatter.28
  276.0 4.9 reduce-scatter.24
  406.5 7.4 reduce-scatter.30
  423.9 7.4 reduce-scatter.26
  441.2 7.4 reduce-scatter.22
  469.0 10.3 reduce-scatter.18
  497.5 10.3 reduce-scatter.44
  515.4 10.3 reduce-scatter.40
  528.6 10.3 reduce-scatter.32
  541.0 10.3 reduce-scatter.36
  622.7 9.4 reduce-scatter.34
  650.6 9.4 reduce-scatter.38
  662.1 9.2 reduce-scatter.42
  674.1 9.2 reduce-scatter.46
Sparse Core Ops, SparseCore 1:
  279.1 57.9 all-gather.6
  339.7 60.4 all-gather.8
where the time goes:
time: 779 us; the launch traced here: 772 us
  blocking collectives  324 us (42%)
  matrix products  197 us (25%)
  waiting for transfers between devices  126 us (16%)
  other arithmetic  82.3 us (11%)
  local copies, waits for them, and re-layouts  22 us (3%)
  between operations  18.7 us (2%)
    psum x1, blocking collectives, local(): adapter_combined = adapter_combined + lax.psum(adapter_portion, 'dp')  77.1 us
    dot_general x28, matrix products, contract_trailing(): lax.dot_general(left, right, (((1,), (1,)), ((), ())), preferred_element_...  53.5 us
    all_gather x1, waiting for transfers between devices, local(): lax.all_gather(feedforward_output_weight, 'dp', axis=1, tiled=True)  52.7 us
    all_gather x1, waiting for transfers between devices, local(): lax.all_gather(feedforward_input_weight, 'dp', axis=0, tiled=True)  47.5 us
    all_gather x1, blocking collectives, local(): lax.all_gather(adapter_down_weight, 'dp', axis=1, tiled=True)  44.5 us
    all_gather x1, blocking collectives, local(): lax.all_gather(key_matrix, 'dp', axis=0, tiled=True)  41.1 us
    all_gather x1, blocking collectives, local(): lax.all_gather(attention_output_weight, 'dp', axis=1, tiled=True)  40.8 us
    all_gather x1, blocking collectives, local(): lax.all_gather(value_matrix, 'dp', axis=0, tiled=True)  39.3 us
  transfers between devices with their start and end apart: 18, of which 6 were waited for; matrix products, arithmetic and copies ran while one was open for 22% of the time, Pallas kernels for 0%

commit v1 on v0

v1 whole, which is shorter than its diff:
```python
import functools

import jax
import jax.numpy as jnp
from jax import lax
from jax.experimental import pallas as pl
from jax.experimental.pallas import tpu as pltpu
from jax.sharding import PartitionSpec as P

F32 = jnp.float32
BF16 = jnp.bfloat16
HEAD_DIM = 64
RANK = 8
LANES = 128
EPS = 1e-05
MASKED = -float(2**30)
SEG = 64
TILE = 256
VMEM_LIMIT = 60 * 2**20

NT = (((1,), (1,)), ((), ()))
TN = (((0,), (0,)), ((), ()))


def mm(a, b):
    return jnp.dot(a, b, preferred_element_type=F32)


def mm_nt(a, b):
    return lax.dot_general(a, b, NT, preferred_element_type=F32)


def mm_tn(a, b):
    return lax.dot_general(a, b, TN, preferred_element_type=F32)


def lane_iota(shape):
    return lax.broadcasted_iota(jnp.int32, shape, len(shape) - 1)


def three_parts(value, lane):
    high = value.astype(BF16).astype(F32)
    rest = value - high
    middle = rest.astype(BF16).astype(F32)
    low = rest - middle
    parts = jnp.where(lane < 16, high, jnp.where(lane < 32, middle, jnp.where(lane < 48, low, 0.0)))
    return parts.astype(BF16)


def two_parts(value):
    high = value.astype(BF16)
    low = (value - high.astype(F32)).astype(BF16)
    return jnp.concatenate([high, low], axis=1)


def load_weights(layout, offsets, pieces, target, sems, columns):
    copies = []
    for group, (first, width) in enumerate(columns):
        for half in range(2):
            for piece, (ref, blocks) in enumerate(zip(pieces[half], layout, strict=True)):
                rows = ref.shape[0] // len(blocks)
                for place, block in enumerate(blocks):
                    start = offsets[block]
                    if rows % 16 == 0:
                        start = pl.multiple_of(start, 16)
                    copies.append(
                        (
                            group,
                            pltpu.make_async_copy(
                                ref.at[pl.ds(place * rows, rows), pl.ds(first, width)],
                                target.at[half, pl.ds(start, rows), pl.ds(first, width)],
                                sems.at[group],
                            ),
                        )
                    )
    return copies


def project_attend_kernel(layout, offsets, lengths, bounds, *refs):
    n = len(layout)
    pieces = (refs[:n], refs[n : 2 * n])
    (
        x_ref,
        bias_ref,
        up_query_ref,
        up_value_ref,
        query_ref,
        key_ref,
        value_ref,
        mixed_ref,
        spare_ref,
        low_ref,
        weights,
        sems,
    ) = refs[2 * n :]
    item = pl.program_id(0)
    half_width = query_ref.shape[2] // 2

    @pl.when(item == 0)
    def _():
        copies = load_weights(layout, offsets, pieces, weights, sems, ((0, weights.shape[2]),))
        for _, copy in copies:
            copy.start()
        for _, copy in copies:
            copy.wait()

    slot = x_ref.shape[1]
    x = x_ref[0]
    low = two_parts(mm(x, weights[0, :, 3 * half_width :]))
    low_ref[0] = low
    for half in range(2):
        at = slice(half * half_width, (half + 1) * half_width)
        query = (
            mm(x, weights[half, :, :half_width])
            + bias_ref[0:1, at]
            + mm(low, up_query_ref[:, at])
        )
        query_ref[0, :, at] = query.astype(BF16) * 0.125
        key_ref[0, :, at] = mm(x, weights[half, :, half_width : 2 * half_width]).astype(BF16)
        value = (
            mm(x, weights[half, :, 2 * half_width : 3 * half_width])
            + bias_ref[1:2, at]
            + mm(low, up_value_ref[:, at])
        )
        value_ref[0, :, at] = value.astype(BF16)

    length = lengths[item]
    bound = bounds[item]
    lane = lane_iota((slot, LANES))
    place = lax.broadcasted_iota(jnp.int32, (slot, LANES), 0)
    second = place >= bound
    flags = jnp.where(
        lane == SEG,
        jnp.where(second, 1.0, 0.0),
        jnp.where(lane == SEG + 1, jnp.where(second, 0.0, 1.0), jnp.where(lane == SEG + 2, 1.0, 0.0)),
    )
    key_flags = jnp.where(
        lane == SEG,
        jnp.where(second, 0.0, MASKED),
        jnp.where(
            lane == SEG + 1,
            jnp.where(second, MASKED, 0.0),
            jnp.where((lane == SEG + 2) & (place >= length), MASKED, 0.0),
        ),
    ).astype(BF16)
    ones = jnp.where(lane == 0, 1.0, 0.0).astype(BF16)
    query_flags = flags.astype(BF16)
    tile_lane = lane_iota((TILE, LANES))
    zero = jnp.zeros((TILE, LANES), BF16)
    logs = [jnp.zeros((TILE, LANES), F32) for _ in range(slot // TILE)]
    for pair in range(2 * half_width // LANES):
        at = slice(pair * LANES, (pair + 1) * LANES)
        keys = jnp.concatenate([key_ref[0, :, at], key_flags], axis=1)
        values = jnp.concatenate([value_ref[0, :, at], ones], axis=1)
        for tile in range(slot // TILE):
            rows = slice(tile * TILE, (tile + 1) * TILE)
            query = query_ref[0, rows, at]
            outs = []
            for side in range(2):
                inside = (tile_lane < HEAD_DIM) if side == 0 else (tile_lane >= HEAD_DIM)
                scores = mm_nt(
                    jnp.concatenate([jnp.where(inside, query, zero), query_flags[rows]], axis=1), keys
                )
                peak = jnp.max(scores, axis=-1, keepdims=True)
                probs = jnp.exp(scores - peak).astype(BF16)
                out = mm(probs, values)
                total = out[:, LANES : LANES + 1]
                outs.append(out[:, :LANES] * (1.0 / total))
                head = 2 * pair + side
                logs[tile] = jnp.where((tile_lane & 15) == head, peak + jnp.log(total), logs[tile])
            mixed_ref[0, rows, at] = jnp.where(tile_lane < HEAD_DIM, outs[0], outs[1]).astype(BF16)
    for tile in range(slot // TILE):
        rows = slice(tile * TILE, (tile + 1) * TILE)
        spare_ref[0, rows] = (
            three_parts(logs[tile], tile_lane).astype(F32) + flags[rows]
        ).astype(BF16)


def row_mean(value):
    return jnp.mean(value, axis=-1, keepdims=True)


def normalize(value):
    centre = value - row_mean(value)
    scale = lax.rsqrt(row_mean(centre * centre) + EPS)
    return centre * scale, scale


def normalize_back(grad, gain, normal, scale):
    grad = grad * gain
    return scale * (grad - row_mean(grad) - normal * row_mean(grad * normal))


def feed_kernel(layout, offsets, *refs):
    n = len(layout)
    pieces = (refs[:n], refs[n : 2 * n])
    (
        x_ref,
        mixed_ref,
        grad_ref,
        hidden_bias_ref,
        output_bias_ref,
        gain_ref,
        shift_ref,
        out_ref,
        grad_hidden_ref,
        grad_mixed_ref,
        weights,
        slope,
        sems,
    ) = refs[2 * n :]
    width = x_ref.shape[1]
    heads = width // 2
    hidden = hidden_bias_ref.shape[1] // 2
    chunk = 512
    first_in = heads
    first_out = heads + hidden

    @pl.when(pl.program_id(0) == 0)
    def _():
        columns = ((0, heads), (first_in, hidden), (first_out, hidden))
        copies = load_weights(layout, offsets, pieces, weights, sems, columns)
        for _, copy in copies:
            copy.start()
        for _, copy in copies:
            copy.wait()

    x = x_ref[...].astype(F32)
    summed = x + output_bias_ref[0:1]
    for half in range(2):
        summed += mm_nt(mixed_ref[:, half * heads : (half + 1) * heads], weights[half, :, :heads])
    normal_in, scale_in = normalize(summed)
    normed = normal_in * gain_ref[0:1] + shift_ref[0:1]
    normed_low = normed.astype(BF16)
    total = normed + output_bias_ref[1:2]
    for half in range(2):
        for part in range(hidden // chunk):
            at = part * chunk
            wide = half * hidden + at
            pre = mm(normed_low, weights[half, :, first_in + at : first_in + at + chunk])
            pre = pre + hidden_bias_ref[:, wide : wide + chunk]
            share = 0.5 * (1.0 + lax.erf(pre * 0.7071067811865476))
            slope[:, wide : wide + chunk] = share + pre * jnp.exp(-0.5 * pre * pre) * 0.3989422804014327
            active = (pre * share).astype(BF16)
            total += mm_nt(active, weights[half, :, first_out + at : first_out + at + chunk])
    normal_out, scale_out = normalize(total)
    out_ref[...] = (normal_out * gain_ref[1:2] + shift_ref[1:2]).astype(BF16)
    grad_total = normalize_back(grad_ref[...].astype(F32), gain_ref[1:2], normal_out, scale_out)
    grad_low = grad_total.astype(BF16)
    grad_normed = grad_total
    for half in range(2):
        for part in range(hidden // chunk):
            at = part * chunk
            wide = half * hidden + at
            grad_active = mm(grad_low, weights[half, :, first_out + at : first_out + at + chunk])
            grad_pre = (grad_active * slope[:, wide : wide + chunk]).astype(BF16)
            grad_normed += mm_nt(grad_pre, weights[half, :, first_in + at : first_in + at + chunk])
    grad_hidden = normalize_back(grad_normed, gain_ref[0:1], normal_in, scale_in)
    grad_hidden_ref[...] = grad_hidden
    grad_hidden_low = grad_hidden.astype(BF16)
    for half in range(2):
        grad_mixed_ref[:, half * heads : (half + 1) * heads] = mm(
            grad_hidden_low, weights[half, :, :heads]
        ).astype(BF16)


def attend_back_kernel(layout, offsets, lengths, bounds, *refs):
    n = len(layout)
    pieces = (refs[:n], refs[n : 2 * n])
    (
        query_ref,
        key_ref,
        value_ref,
        mixed_ref,
        spare_ref,
        low_ref,
        grad_mixed_ref,
        grad_hidden_ref,
        up_query_ref,
        up_value_ref,
        out_ref,
        adapter_ref,
        weights,
        grad_query,
        grad_key,
        grad_value,
        sems,
    ) = refs[2 * n :]
    item = pl.program_id(0)
    slot, width = query_ref.shape[1:]
    half_width = width // 2

    @pl.when(item == 0)
    def _():
        copies = load_weights(layout, offsets, pieces, weights, sems, ((0, weights.shape[2]),))
        for _, copy in copies:
            copy.start()
        for _, copy in copies:
            copy.wait()

    length = lengths[item]
    bound = bounds[item]
    lane = lane_iota((slot, LANES))
    place = lax.broadcasted_iota(jnp.int32, (slot, LANES), 0)
    second = place >= bound
    key_flags = jnp.where(
        lane == SEG,
        jnp.where(second, 0.0, MASKED),
        jnp.where(
            lane == SEG + 1,
            jnp.where(second, MASKED, 0.0),
            jnp.where((lane == SEG + 2) & (place >= length), MASKED, 0.0),
        ),
    )
    row = lax.broadcasted_iota(jnp.int32, (width, LANES), 0)
    column = lane_iota((width, LANES))
    pick = jnp.where((row // HEAD_DIM == (column & 15)) & (column < 48), 1.0, 0.0).astype(BF16)
    product = grad_mixed_ref[0].astype(F32) * mixed_ref[0].astype(F32)
    high = product.astype(BF16)
    rest = (product - high.astype(F32)).astype(BF16)
    inner = three_parts(mm(high, pick) + mm(rest, pick), lane)
    spare = spare_ref[0]
    low_side = lane < HEAD_DIM
    zero = jnp.zeros((slot, LANES), BF16)
    for pair in range(width // LANES):
        at = slice(pair * LANES, (pair + 1) * LANES)
        query = query_ref[0, :, at]
        keys = key_ref[0, :, at]
        values = value_ref[0, :, at]
        grad = grad_mixed_ref[0, :, at]
        total_query = jnp.zeros((slot, LANES), F32)
        total_key = jnp.zeros((slot, LANES), F32)
        total_value = jnp.zeros((slot, LANES), F32)
        for side in range(2):
            head = 2 * pair + side
            inside = low_side if side == 0 else lane >= HEAD_DIM
            mine = ((lane & 15) == head) & (lane < 48)
            query_side = jnp.where(inside, query, zero)
            key_side = jnp.where(inside, keys, zero)
            grad_side = jnp.where(inside, grad, zero)
            key_wide = jnp.concatenate([keys, jnp.where(mine, -1.0, key_flags).astype(BF16)], axis=1)
            value_wide = jnp.concatenate([values, jnp.where(mine, -1.0, 0.0).astype(BF16)], axis=1)
            probs = jnp.exp(mm_nt(key_wide, jnp.concatenate([query_side, spare], axis=1)))
            grad_probs = mm_nt(value_wide, jnp.concatenate([grad_side, inner], axis=1))
            grad_scores = (probs * grad_probs).astype(BF16)
            total_value += mm(probs.astype(BF16), grad_side)
            total_key += mm(grad_scores, query_side)
            total_query += mm_tn(grad_scores, key_side)
        grad_query[:, at] = (total_query * 0.125).astype(BF16)
        grad_key[:, at] = total_key.astype(BF16)
        grad_value[:, at] = total_value.astype(BF16)

    small = mm_nt(grad_query[...], up_query_ref[:LANES]) + mm_nt(grad_value[...], up_value_ref[:LANES])
    down = weights[0, :, 3 * half_width :]
    total = grad_hidden_ref[0] + mm_nt(two_parts(small), jnp.concatenate([down, down], axis=1))
    for half in range(2):
        at = slice(half * half_width, (half + 1) * half_width)
        for index, grads in enumerate((grad_query, grad_key, grad_value)):
            total += mm_nt(
                grads[:, at], weights[half, :, index * half_width : (index + 1) * half_width]
            )
    out_ref[0] = total
    low = low_ref[0]
    by_query = mm_tn(low, grad_query[...])
    by_value = mm_tn(low, grad_value[...])
    update = 2.0 * jnp.concatenate(
        [
            by_query[:RANK] + by_query[LANES : LANES + RANK],
            by_value[RANK : 2 * RANK] + by_value[LANES + RANK : LANES + 2 * RANK],
        ],
        axis=0,
    )

    @pl.when(item == 0)
    def _():
        adapter_ref[...] = update

    @pl.when(item > 0)
    def _():
        adapter_ref[...] += update


def any_spec():
    return pl.BlockSpec(memory_space=pl.ANY)


def whole_spec(array):
    return pl.BlockSpec(array.shape, lambda i, *_: (0,) * array.ndim)


def item_spec(shape):
    return pl.BlockSpec((1, *shape[1:]), lambda i, *_: (i, 0, 0))


def shape_of(shape, dtype):
    return jax.ShapeDtypeStruct(shape, dtype)


def project_attend(layout, offsets, lengths, bounds, pieces, x, bias, up_query, up_value):
    items, slot, width = x.shape
    flat = [*pieces[0], *pieces[1]]
    columns = pieces[0][0].shape[1]
    outs = [shape_of(x.shape, BF16)] * 4 + [
        shape_of((items, slot, LANES), BF16),
        shape_of((items, slot, 2 * LANES), BF16),
    ]
    flops = 2 * items * slot * width * (3 * width + 4 * slot)
    return pl.pallas_call(
        functools.partial(project_attend_kernel, layout),
        grid_spec=pltpu.PrefetchScalarGridSpec(
            num_scalar_prefetch=3,
            grid=(items,),
            in_specs=[any_spec()] * len(flat)
            + [item_spec(x.shape), whole_spec(bias), whole_spec(up_query), whole_spec(up_value)],
            out_specs=[item_spec(out.shape) for out in outs],
            scratch_shapes=[
                pltpu.VMEM((2, width, columns), BF16),
                pltpu.SemaphoreType.DMA((1,)),
            ],
        ),
        out_shape=outs,
        compiler_params=pltpu.CompilerParams(vmem_limit_bytes=VMEM_LIMIT),
        cost_estimate=pl.CostEstimate(
            flops=flops, bytes_accessed=12 * items * slot * width, transcendentals=items * slot * slot * 12
        ),
        name="project_attend",
    )(offsets, lengths, bounds, *flat, x, bias, up_query, up_value)


def feed(layout, offsets, pieces, x, mixed, grad, hidden_bias, output_bias, gain, shift):
    rows, width = x.shape
    flat = [*pieces[0], *pieces[1]]
    columns = pieces[0][0].shape[1]
    tile = pl.BlockSpec((TILE, width), lambda i, *_: (i, 0))
    outs = [shape_of(x.shape, BF16), shape_of(x.shape, F32), shape_of(x.shape, BF16)]
    smalls = (hidden_bias, output_bias, gain, shift)
    return pl.pallas_call(
        functools.partial(feed_kernel, layout),
        grid_spec=pltpu.PrefetchScalarGridSpec(
            num_scalar_prefetch=1,
            grid=(rows // TILE,),
            in_specs=[any_spec()] * len(flat) + [tile] * 3 + [whole_spec(a) for a in smalls],
            out_specs=[tile] * 3,
            scratch_shapes=[
                pltpu.VMEM((2, width, columns), BF16),
                pltpu.VMEM((TILE, hidden_bias.shape[1]), F32),
                pltpu.SemaphoreType.DMA((3,)),
            ],
        ),
        out_shape=outs,
        compiler_params=pltpu.CompilerParams(vmem_limit_bytes=VMEM_LIMIT),
        cost_estimate=pl.CostEstimate(
            flops=8 * rows * width * columns, bytes_accessed=4 * width * columns, transcendentals=0
        ),
        name="feed",
    )(offsets, *flat, x, mixed, grad, *smalls)


def attend_back(layout, offsets, lengths, bounds, pieces, query, key, value, mixed, spare, low, grad_mixed, grad_hidden, up_query, up_value):
    items, slot, width = query.shape
    flat = [*pieces[0], *pieces[1]]
    columns = pieces[0][0].shape[1]
    blocks = (query, key, value, mixed, spare, low, grad_mixed, grad_hidden)
    adapter = (2 * RANK, width)
    return pl.pallas_call(
        functools.partial(attend_back_kernel, layout),
        grid_spec=pltpu.PrefetchScalarGridSpec(
            num_scalar_prefetch=3,
            grid=(items,),
            in_specs=[any_spec()] * len(flat)
            + [item_spec(a.shape) for a in blocks]
            + [whole_spec(up_query), whole_spec(up_value)],
            out_specs=[item_spec(query.shape), pl.BlockSpec(adapter, lambda i, *_: (0, 0))],
            scratch_shapes=[
                pltpu.VMEM((2, width, columns), BF16),
                pltpu.VMEM((slot, width), BF16),
                pltpu.VMEM((slot, width), BF16),
                pltpu.VMEM((slot, width), BF16),
                pltpu.SemaphoreType.DMA((1,)),
            ],
        ),
        out_shape=[shape_of(query.shape, F32), shape_of(adapter, F32)],
        compiler_params=pltpu.CompilerParams(vmem_limit_bytes=VMEM_LIMIT),
        cost_estimate=pl.CostEstimate(
            flops=2 * items * slot * width * (3 * width + 10 * slot),
            bytes_accessed=16 * items * slot * width,
            transcendentals=items * slot * slot * 12,
        ),
        name="attend_back",
    )(offsets, lengths, bounds, *flat, *blocks, up_query, up_value)


def swap(array):
    return lax.ppermute(array, "tensor", [(0, 1), (1, 0)])


def ring_gather(shard, count):
    def moved(array, target):
        return lax.ppermute(array, "dp", [(i, target(i)) for i in range(count)])

    plane = [shard] + [moved(shard, lambda i, d=d: (i + 4 * d) % count) for d in (1, 2, 3)]
    line = jnp.concatenate(plane, axis=0)
    half = line.shape[0] // 2
    by_x = moved(line, lambda i: i ^ 1)
    by_y = moved(line, lambda i: i ^ 2)
    far_low = moved(by_x[:half], lambda i: i ^ 2)
    far_high = moved(by_y[half:], lambda i: i ^ 1)
    return [line, by_x, by_y, far_low, far_high]


RING_LAYOUT = ((0, 1, 2, 3), (4, 5, 6, 7), (8, 9, 10, 11), (12, 13), (14, 15))


def ring_offsets(index, rows):
    table = []
    for flip in (0, 1, 2, 3):
        for back in range(4):
            table.append((((index ^ flip) - 4 * back) % 16) * rows)
    return jnp.stack(table).astype(jnp.int32)


def local(
    inputs,
    lengths,
    bounds,
    query_matrix,
    key_matrix,
    value_matrix,
    query_value_bias,
    adapter_down_weight,
    adapter_up_weight,
    attention_output_weight,
    feedforward_input_weight,
    feedforward_input_bias,
    feedforward_output_weight,
    output_bias,
    layernorm_scale,
    layernorm_bias,
    output_gradient,
    *,
    count,
):
    micro, rows, width = inputs.shape
    mine = micro // 2
    core = lax.axis_index("tensor")
    shard_rows = query_matrix.shape[0]

    down = jnp.transpose(adapter_down_weight, (1, 0, 2)).reshape(shard_rows, 2 * RANK)
    down = jnp.pad(down, ((0, 0), (0, LANES - 2 * RANK)))
    shard = jnp.concatenate([query_matrix, key_matrix, value_matrix, down], axis=1)
    shard_feed = jnp.concatenate(
        [attention_output_weight.T, feedforward_input_weight, feedforward_output_weight.T], axis=1
    )
    zero = jnp.zeros((1,), jnp.int32)
    if count == 16:
        offsets = ring_offsets(lax.axis_index("dp"), shard_rows)
        layout = RING_LAYOUT
        own = ring_gather(shard, count)
    else:
        offsets = zero
        layout = ((0,),)
        own = [lax.all_gather(shard, "dp", axis=0, tiled=True)]
    pieces = (own, [swap(piece) for piece in own])
    own_feed = [lax.all_gather(shard_feed, "dp", axis=0, tiled=True)]
    pieces_feed = (own_feed, [swap(piece) for piece in own_feed])

    first = core * mine
    other_first = (1 - core) * mine

    def take_items(array):
        kept = lax.dynamic_slice_in_dim(array, first, mine, 0)
        given = lax.dynamic_slice_in_dim(array, other_first, mine, 0)
        got = swap(given)
        return jnp.where(
            core == 0,
            jnp.concatenate([kept, got], axis=1),
            jnp.concatenate([got, kept], axis=1),
        )

    def give_items(array):
        kept = lax.dynamic_slice_in_dim(array, core * rows, rows, 1)
        given = lax.dynamic_slice_in_dim(array, (1 - core) * rows, rows, 1)
        got = swap(given)
        return jnp.where(
            core == 0,
            jnp.concatenate([kept, got], axis=0),
            jnp.concatenate([got, kept], axis=0),
        )

    x = take_items(inputs)
    grad = take_items(output_gradient)
    my_lengths = lax.dynamic_slice_in_dim(lengths[:, 0], first, mine, 0)
    my_bounds = lax.dynamic_slice_in_dim(bounds[:, 0], first, mine, 0)

    bias = jnp.concatenate([query_value_bias, swap(query_value_bias)], axis=1)
    hidden_bias = feedforward_input_bias[None]
    hidden_bias = jnp.concatenate([hidden_bias, swap(hidden_bias)], axis=1)
    up = jnp.concatenate([adapter_up_weight, swap(adapter_up_weight)], axis=2) * 2
    up_query = jnp.pad(up[0], ((0, LANES - RANK), (0, 0)))
    up_value = jnp.pad(up[1], ((RANK, LANES - 2 * RANK), (0, 0)))
    up_query = jnp.concatenate([up_query, up_query], axis=0)
    up_value = jnp.concatenate([up_value, up_value], axis=0)

    query, key, value, mixed, spare, low = project_attend(
        layout, offsets, my_lengths, my_bounds, pieces, x, bias, up_query, up_value
    )
    flat = (mine * 2 * rows, width)
    out, grad_hidden, grad_mixed = feed(
        ((0,),),
        zero,
        pieces_feed,
        x.reshape(flat),
        mixed.reshape(flat),
        grad.reshape(flat),
        hidden_bias,
        output_bias,
        layernorm_scale,
        layernorm_bias,
    )
    input_grad, adapter = attend_back(
        layout,
        offsets,
        my_lengths,
        my_bounds,
        pieces,
        query,
        key,
        value,
        mixed,
        spare,
        low,
        grad_mixed.reshape(x.shape),
        grad_hidden.reshape(x.shape),
        up_query,
        up_value,
    )
    half = width // 2
    adapter = adapter[:, :half] + swap(adapter[:, half:])
    adapter = lax.psum(adapter, "dp").reshape(2, RANK, half)
    return give_items(out.reshape(x.shape)), give_items(input_grad), adapter


def solution(mesh):
    return jax.shard_map(
        functools.partial(local, count=mesh.shape["dp"]),
        mesh=mesh,
        in_specs=(
            P(None, ("dp", "tensor"), None),
            P(None, "dp"),
            P(None, "dp"),
            P("dp", "tensor"),
            P("dp", "tensor"),
            P("dp", "tensor"),
            P(None, "tensor"),
            P(None, "dp", None),
            P(None, None, "tensor"),
            P("tensor", "dp"),
            P("dp", "tensor"),
            P("tensor"),
            P("tensor", "dp"),
            P(),
            P(),
            P(),
            P(None, ("dp", "tensor"), None),
        ),
        out_specs=(
            P(None, ("dp", "tensor"), None),
            P(None, ("dp", "tensor"), None),
            P(None, None, "tensor"),
        ),
        check_vma=False,
    )
```

time: 779 us -> 383 us (0.49); the launches traced: 772 us -> 386 us
  blocking collectives: 324 us -> 73.6 us
  matrix products: 197 us -> 0 us
  Pallas kernels: 0 us -> 133 us
  other arithmetic: 82.3 us -> 19.3 us
  local copies, waits for them, and re-layouts: 22 us -> 8.58 us
  starting transfers between devices: 1.37 us -> 11.7 us
    all_gather x21 -> x0, blocking collectives: 247 us -> none  [the longest x1 44.5 us: local(): lax.all_gather(adapter_down_weight, 'dp', axis=1, tiled=True)]
    dot_general x104 -> x0, matrix products: 197 us -> none  [the longest x28 53.5 us: contract_trailing(): lax.dot_general(left, right, (((1,), (1,)), ((), ())), preferred_element_...]
    pallas_call x0 -> x3, Pallas kernels: none -> 133 us  [the longest x1 57.3 us: feed(): pl.pallas_call(functools.partial(feed_kernel, layout), grid_spec=pltpu.Pr...]
    ppermute x0 -> x21, waiting for transfers between devices: none -> 35.4 us  [the longest x7 27.9 us: moved(): return lax.ppermute(array, 'dp', [(i, target(i)) for i in range(count)])]
    reduce_sum x18 -> x0, other arithmetic: 33.6 us -> none  [the longest x8 19.8 us: layer_norm(): centre = value_rows - jnp.mean(value_rows, axis=-1, keepdims=True)]
    convert_element_type x13 -> x0, other arithmetic: 26.4 us -> none  [the longest x4 22.9 us: attend_backward(): grad_scores = (probs * (grad_probs - inner)).astype(jnp.bfloat16)]
    reduce_scatter x16 -> x0, waiting for transfers between devices: 25 us -> none  [the longest x4 16.1 us: forward_pass(): lax.psum_scatter(jnp.dot(activated, ffn_out_full, preferred_element_type=...]
    unnamed x429 -> x34, local copies, waits for them, and re-layouts: 15.9 us -> 1.78 us
  transfers between devices with their start and end apart: 18 -> 22, of which waited for: 6 -> 10; matrix products, arithmetic and copies ran while one was open for 22% -> 4% of each run, Pallas kernels for 0% -> 9%
where the time goes in v1:
time: 383 us; the launch traced here: 386 us
  Pallas kernels  133 us (35%)
  waiting for transfers between devices  126 us (33%)
  blocking collectives  73.6 us (19%)
  other arithmetic  19.3 us (5%)
  between operations  14.5 us (4%)
  starting transfers between devices  11.7 us (3%)
  local copies, waits for them, and re-layouts  8.58 us (2%)
    all_gather x1, waiting for transfers between devices, local(): own_feed = [lax.all_gather(shard_feed, 'dp', axis=0, tiled=True)]  90.1 us
    psum x1, blocking collectives, local(): adapter = lax.psum(adapter, 'dp').reshape(2, RANK, half)  73.6 us
    pallas_call x1, Pallas kernels, feed(): pl.pallas_call(functools.partial(feed_kernel, layout), grid_spec=pltpu.Pr...  57.3 us
    pallas_call x1, Pallas kernels, attend_back(): pl.pallas_call(functools.partial(attend_back_kernel, layout), grid_spec=p...  41.2 us
    pallas_call x1, Pallas kernels, project_attend(): pl.pallas_call(functools.partial(project_attend_kernel, layout), grid_spe...  34.6 us
    ppermute x7, waiting for transfers between devices, moved(): return lax.ppermute(array, 'dp', [(i, target(i)) for i in range(count)])  27.9 us
    ppermute x7, starting transfers between devices, moved(): return lax.ppermute(array, 'dp', [(i, target(i)) for i in range(count)])  9.16 us
  transfers between devices with their start and end apart: 22, of which 10 were waited for; matrix products, arithmetic and copies ran while one was open for 4% of the time, Pallas kernels for 9%

profile of v1, /device:TPU:0, one launch (start us, length us, event | category | flops | bytes accessed | tf_op | source)
XLA Modules:
  0.0 386.4 jit_solution(10063796356162943113)
XLA Ops:
  7.2 1.8 pad_maximum_fusion.3
  9.1 90.1 %all-gather.2.cloned.1.call-done.refs_0_ = bf16[768,3456]{1,0:T(8,128)(2,1)} async-done(((bf16[48,3456]{1,0:T(8,128)(2,1)}), bf16[768,3456]{1,0:T(8,128)(2,1)}) %all-gather.2.cloned.1.call-update) | async-done | bytes 5308432 | tf_op jit(solution)/shard_map/all_gather | solution.py:564
  100.8 2.1 collective-permute-start.4
  104.9 1.8 collective-permute-done.4
  106.7 8.7 %collective-permute-done.3 = bf16[48,1280]{1,0:T(8,128)(2,1)S(1)} collective-permute-done((bf16[48,1280]{1,0:T(8,128)(2,1)S(1)}, bf16[48,1280]{1,0:T(8,128)(2,1)S(1)}, u32[]{:S(2)}, u32[]{:S(2)}) %collective-permute-start.3) | collective-permute-done | bytes 122912 | tf_op jit(solution)/shard_map/ppermute | solution.py:499
  115.4 1.6 pad_maximum_fusion.refs_0_
  117.0 1.5 collective-permute-start.6
  119.5 2.8 collective-permute-done.14
  125.2 4.9 %collective-permute-done.6.refs_2_ = bf16[192,1280]{1,0:T(8,128)(2,1)} collective-permute-done((bf16[192,1280]{1,0:T(8,128)(2,1)}, bf16[192,1280]{1,0:T(8,128)(2,1)}, u32[]{:S(2)}, u32[]{:S(2)}) %collective-permute-start.6) | collective-permute-done | bytes 491552 | tf_op jit(solution)/shard_map/ppermute | solution.py:499
  130.1 1.4 collective-permute-start.5
  133.8 8.5 %collective-permute-done.5.refs_1_ = bf16[192,1280]{1,0:T(8,128)(2,1)S(1)} collective-permute-done((bf16[192,1280]{1,0:T(8,128)(2,1)}, bf16[192,1280]{1,0:T(8,128)(2,1)S(1)}, u32[]{:S(2)}, u32[]{:S(2)}) %collective-permute-start.5) | collective-permute-done | bytes 491552 | tf_op jit(solution)/shard_map/ppermute | solution.py:499
  142.3 1.4 collective-permute-start.8
  146.0 2.5 collective-permute-done.8.refs_4_
  148.5 1.5 collective-permute-done.7.refs_3_
  150.0 3.1 maximum_select_fusion.1.refs_10_
  153.1 3.1 maximum_select_fusion.2
  157.4 34.6 %project_attend.1 = (bf16[2,512,768]{2,1,0:T(8,128)(2,1)}, bf16[2,512,768]{2,1,0:T(8,128)(2,1)}, bf16[2,512,768]{2,1,0:T(8,128)(2,1)}, bf16[2,512,768]{2,1,0:T(8...) custom-call(s32[16]{0:T(128)} %stack.67.offsets, s32[2]{0:T(128)} %get-tuple-element.35.lengths, ...), custom_call_target="tpu_custom_call" | custom-call | flops 6845104128 | bytes 9437184 | tf_op jit(solution)/shard_map/project_attend/pallas_call | solution.py:408
  192.1 57.3 %feed.1 = (bf16[1024,768]{1,0:T(8,128)(2,1)}, f32[1024,768]{1,0:T(8,128)}, bf16[1024,768]{1,0:T(8,128)(2,1)}) custom-call(s32[1]{0:T(128)} %constant.105.clone.1.offsets, bf16[768,3456]{1,0:T(8,128)(2,1)} %all-gather.2.cloned.1.call-done.refs_0_, bf16[768,3456]{1,0:T(8,128)(2,1)} %collective-permute-done.refs_1_, bf16[1024,768]{1,0:T(8,128)(2,1)} %bitcast.38, ...), custom_call_target="tpu_custom_call" | custom-call | flops 21743271936 | bytes 10616832 | tf_op jit(solution)/shard_map/feed/pallas_call | solution.py:437
  249.4 41.2 %attend_back.1 = (f32[2,512,768]{2,1,0:T(8,128)}, f32[16,768]{1,0:T(8,128)}) custom-call(s32[16]{0:T(128)} %stack.67.offsets, s32[2]{0:T(128)} %get-tuple-element.35.lengths, s32[2]{0:T(128)} %get-tuple-element.36.bounds, bf16[192,1280]{1,0:T(8,128)(2,1)} %pad_maximum_fusion.refs_0_, bf16[192,1280]{1,0:T(8,128)(2,1)} %copy-done.3, ...), custom_call_target="tpu_custom_call" | custom-call | flops 11676942336 | bytes 12582912 | tf_op jit(solution)/shard_map/attend_back/pallas_call | solution.py:465
  290.7 3.4 constant_dynamic-slice_fusion.1
  295.5 3.6 collective-permute-done.20
  299.1 73.6 %psum.7 = f32[2,8,384]{2,1,0:T(8,128)} all-reduce(f32[2,8,384]{2,1,0:T(8,128)S(1)} %add_bitcast_fusion), channel_id=1, replica_groups=mesh['dp'=16,'tensor'=2] {'dp'}, use_global_device_ids=true, to_apply=%region_0.1 | all-reduce | flops 6144 | bytes 49152 | tf_op jit(solution)/shard_map/psum | solution.py:639
  372.7 2.8 maximum_select_fusion.3
  375.5 3.9 %maximum_select_fusion = f32[4,256,768]{2,1,0:T(8,128)} fusion(f32[2,256,768]{2,1,0:T(8,128)} %collective-permute-done.19, f32[2,256,768]{2,1,0:T(8,128)S(1)} %get-tuple-element.25, pred[]{:T(512)S(6)} %eq.23), kind=kLoop, calls=%fused_computation | loop fusion | flops 2359296 | bytes 6291457 | tf_op jit(solution)/shard_map/jit(_where)/select_n | solution.py:584
  (86 shorter events, 14.4 us)
Async XLA Ops:
  7.2 111.4 %copy-start = (bf16[4,256,768]{2,1,0:T(8,128)(2,1)S(1)}, bf16[4,256,768]{2,1,0:T(8,128)(2,1)}, u32[]{:S(2)}) copy-start(bf16[4,256,768]{2,1,0:T(8,128)(2,1)} %param.17) | copy-start | bytes 4718596
  7.2 92.0 %all-gather.2.cloned.1.call-start = ((), (), s32[]{:S(2)}) async-start(), calls=%async_computation | async-start | bytes 5640192 | tf_op jit(solution)/shard_map/all_gather | solution.py:564
  99.2 92.9 %collective-permute-start = (bf16[768,3456]{1,0:T(8,128)(2,1)}, bf16[768,3456]{1,0:T(8,128)(2,1)}, u32[]{:S(2)}, u32[]{:S(2)}) collective-permute-start(bf16[768,3456]{1,0:T(8,128)(2,1)} %all-gather.2.cloned.1.call-done.refs_0_), channel_id=1, source_target_pairs={{0,1},{1,0},{2,3},{3,2},{4,5},{5,4},{6,7},{7,6},{8,9},{9,8},{10,11... | collective-permute-start | bytes 15925256 | tf_op jit(solution)/shard_map/ppermute | solution.py:494
  100.8 5.9 %collective-permute-start.4 = (bf16[48,1280]{1,0:T(8,128)(2,1)S(1)}, bf16[48,1280]{1,0:T(8,128)(2,1)S(1)}, u32[]{:S(2)}, u32[]{:S(2)}) collective-permute-start(bf16[48,1280]{1,0:T(8,128)(2,1)S(1)} %pad_maximum_fusion.4), channel_id=1, source_target_pairs={{0,24},{2,26},{4,28},{6,30},{8,0},{10,2},{12,4},{14,6},{16,8},{18,... | collective-permute-start | bytes 368648 | tf_op jit(solution)/shard_map/ppermute | solution.py:499
  102.9 12.5 %collective-permute-start.3 = (bf16[48,1280]{1,0:T(8,128)(2,1)S(1)}, bf16[48,1280]{1,0:T(8,128)(2,1)S(1)}, u32[]{:S(2)}, u32[]{:S(2)}) collective-permute-start(bf16[48,1280]{1,0:T(8,128)(2,1)S(1)} %pad_maximum_fusion.4), channel_id=1, source_target_pairs={{0,16},{2,18},{4,20},{6,22},{8,24},{10,26},{12,28},{14,30},{16,0},... | collective-permute-start | bytes 368648 | tf_op jit(solution)/shard_map/ppermute | solution.py:499
  103.8 11.6 %collective-permute-start.2 = (bf16[48,1280]{1,0:T(8,128)(2,1)S(1)}, bf16[48,1280]{1,0:T(8,128)(2,1)S(1)}, u32[]{:S(2)}, u32[]{:S(2)}) collective-permute-start(bf16[48,1280]{1,0:T(8,128)(2,1)S(1)} %pad_maximum_fusion.4), channel_id=1, source_target_pairs={{0,8},{2,10},{4,12},{6,14},{8,16},{10,18},{12,20},{14,22},{16,24},... | collective-permute-start | bytes 368648 | tf_op jit(solution)/shard_map/ppermute | solution.py:499
  117.0 13.1 %collective-permute-start.6 = (bf16[192,1280]{1,0:T(8,128)(2,1)}, bf16[192,1280]{1,0:T(8,128)(2,1)}, u32[]{:S(2)}, u32[]{:S(2)}) collective-permute-start(bf16[192,1280]{1,0:T(8,128)(2,1)} %pad_maximum_fusion.refs_0_), channel_id=1, source_target_pairs={{0,4},{2,6},{4,0},{6,2},{8,12},{10,14},{12,8},{14,10},{16,20},{18,... | collective-permute-start | bytes 1474568 | tf_op jit(solution)/shard_map/ppermute | solution.py:499
  118.7 25.7 %collective-permute-start.1 = (bf16[2,256,768]{2,1,0:T(8,128)(2,1)S(1)}, bf16[2,256,768]{2,1,0:T(8,128)(2,1)}, u32[]{:S(2)}, u32[]{:S(2)}) collective-permute-start(bf16[2,256,768]{2,1,0:T(8,128)(2,1)S(1)} %get-tuple-element.32), channel_id=1, source_target_pairs={{0,1},{1,0},{2,3},{3,2},{4,5},{5,4},{6,7},{7,6},{8,9},{9,8},{10,11... | collective-permute-start | bytes 2359304 | tf_op jit(solution)/shard_map/ppermute | solution.py:494
  118.9 25.5 %collective-permute-start.16 = (bf16[2,256,768]{2,1,0:T(8,128)(2,1)S(1)}, bf16[2,256,768]{2,1,0:T(8,128)(2,1)}, u32[]{:S(2)}, u32[]{:S(2)}) collective-permute-start(bf16[2,256,768]{2,1,0:T(8,128)(2,1)S(1)} %get-tuple-element.30), channel_id=1, source_target_pairs={{0,1},{1,0},{2,3},{3,2},{4,5},{5,4},{6,7},{7,6},{8,9},{9,8},{10,11... | collective-permute-start | bytes 2359304 | tf_op jit(solution)/shard_map/ppermute | solution.py:494
  119.4 2.9 collective-permute-start.14
  122.3 1.2 collective-permute-start.17
  123.5 1.4 collective-permute-start.15
  124.9 18.9 %collective-permute-start.9 = (bf16[192,1280]{1,0:T(8,128)(2,1)}, bf16[192,1280]{1,0:T(8,128)(2,1)S(1)}, u32[]{:S(2)}, u32[]{:S(2)}) collective-permute-start(bf16[192,1280]{1,0:T(8,128)(2,1)} %pad_maximum_fusion.refs_0_), channel_id=1, source_target_pairs={{0,1},{1,0},{2,3},{3,2},{4,5},{5,4},{6,7},{7,6},{8,9},{9,8},{10,11... | collective-permute-start | bytes 1474568 | tf_op jit(solution)/shard_map/ppermute | solution.py:494
  130.1 12.1 %collective-permute-start.5 = (bf16[192,1280]{1,0:T(8,128)(2,1)}, bf16[192,1280]{1,0:T(8,128)(2,1)S(1)}, u32[]{:S(2)}, u32[]{:S(2)}) collective-permute-start(bf16[192,1280]{1,0:T(8,128)(2,1)} %pad_maximum_fusion.refs_0_), channel_id=1, source_target_pairs={{0,2},{2,0},{4,6},{6,4},{8,10},{10,8},{12,14},{14,12},{16,18},{18,... | collective-permute-start | bytes 1474568 | tf_op jit(solution)/shard_map/ppermute | solution.py:499
  142.3 10.9 %copy-start.3 = (bf16[192,1280]{1,0:T(8,128)(2,1)}, bf16[192,1280]{1,0:T(8,128)(2,1)S(1)}, u32[]{:S(2)}) copy-start(bf16[192,1280]{1,0:T(8,128)(2,1)S(1)} %collective-permute-done.5.refs_1_) | copy-start | bytes 1474564
  142.3 6.2 %collective-permute-start.8 = (bf16[96,1280]{1,0:T(8,128)(2,1)S(1)}, bf16[96,1280]{1,0:T(8,128)(2,1)S(1)}, u32[]{:S(2)}, u32[]{:S(2)}) collective-permute-start(bf16[96,1280]{1,0:T(8,128)(2,1)S(1)} %slice.25), channel_id=1, source_target_pairs={{0,2},{2,0},{4,6},{6,4},{8,10},{10,8},{12,14},{14,12},{16,18},{18,... | collective-permute-start | bytes 737288 | tf_op jit(solution)/shard_map/ppermute | solution.py:499
  143.8 6.3 %collective-permute-start.7 = (bf16[96,1280]{1,0:T(8,128)(2,1)S(1)}, bf16[96,1280]{1,0:T(8,128)(2,1)S(1)}, u32[]{:S(2)}, u32[]{:S(2)}) collective-permute-start(bf16[96,1280]{1,0:T(8,128)(2,1)S(1)} %slice.24), channel_id=1, source_target_pairs={{0,4},{2,6},{4,0},{6,2},{8,12},{10,14},{12,8},{14,10},{16,20},{18,... | collective-permute-start | bytes 737288 | tf_op jit(solution)/shard_map/ppermute | solution.py:499
  144.4 11.8 %collective-permute-start.11 = (bf16[192,1280]{1,0:T(8,128)(2,1)}, bf16[192,1280]{1,0:T(8,128)(2,1)S(1)}, u32[]{:S(2)}, u32[]{:S(2)}) collective-permute-start(bf16[192,1280]{1,0:T(8,128)(2,1)} %collective-permute-done.6.refs_2_), channel_id=1, source_target_pairs={{0,1},{1,0},{2,3},{3,2},{4,5},{5,4},{6,7},{7,6},{8,9},{9,8},{10,11... | collective-permute-start | bytes 1474568 | tf_op jit(solution)/shard_map/ppermute | solution.py:494
  144.4 11.8 %collective-permute-start.10 = (bf16[192,1280]{1,0:T(8,128)(2,1)S(1)}, bf16[192,1280]{1,0:T(8,128)(2,1)S(1)}, u32[]{:S(2)}, u32[]{:S(2)}) collective-permute-start(bf16[192,1280]{1,0:T(8,128)(2,1)S(1)} %collective-permute-done.5.refs_1_), channel_id=1, source_target_pairs={{0,1},{1,0},{2,3},{3,2},{4,5},{5,4},{6,7},{7,6},{8,9},{9,8},{10,11... | collective-permute-start | bytes 1474568 | tf_op jit(solution)/shard_map/ppermute | solution.py:494
  148.5 7.8 %collective-permute-start.13 = (bf16[96,1280]{1,0:T(8,128)(2,1)S(1)}, bf16[96,1280]{1,0:T(8,128)(2,1)S(1)}, u32[]{:S(2)}, u32[]{:S(2)}) collective-permute-start(bf16[96,1280]{1,0:T(8,128)(2,1)S(1)} %collective-permute-done.8.refs_4_), channel_id=1, source_target_pairs={{0,1},{1,0},{2,3},{3,2},{4,5},{5,4},{6,7},{7,6},{8,9},{9,8},{10,11... | collective-permute-start | bytes 737288 | tf_op jit(solution)/shard_map/ppermute | solution.py:494
  150.0 6.2 %collective-permute-start.12 = (bf16[96,1280]{1,0:T(8,128)(2,1)S(1)}, bf16[96,1280]{1,0:T(8,128)(2,1)S(1)}, u32[]{:S(2)}, u32[]{:S(2)}) collective-permute-start(bf16[96,1280]{1,0:T(8,128)(2,1)S(1)} %collective-permute-done.7.refs_3_), channel_id=1, source_target_pairs={{0,1},{1,0},{2,3},{3,2},{4,5},{5,4},{6,7},{7,6},{8,9},{9,8},{10,11... | collective-permute-start | bytes 737288 | tf_op jit(solution)/shard_map/ppermute | solution.py:494
  294.2 81.3 %collective-permute-start.19 = (f32[2,256,768]{2,1,0:T(8,128)}, f32[2,256,768]{2,1,0:T(8,128)}, u32[]{:S(2)}, u32[]{:S(2)}) collective-permute-start(f32[2,256,768]{2,1,0:T(8,128)} %get-tuple-element.26), channel_id=1, source_target_pairs={{0,1},{1,0},{2,3},{3,2},{4,5},{5,4},{6,7},{7,6},{8,9},{9,8},{10,11... | collective-permute-start | bytes 4718600 | tf_op jit(solution)/shard_map/ppermute | solution.py:494
  294.7 78.0 %collective-permute-start.18 = (bf16[2,256,768]{2,1,0:T(8,128)(2,1)S(1)}, bf16[2,256,768]{2,1,0:T(8,128)(2,1)}, u32[]{:S(2)}, u32[]{:S(2)}) collective-permute-start(bf16[2,256,768]{2,1,0:T(8,128)(2,1)S(1)} %get-tuple-element.28), channel_id=1, source_target_pairs={{0,1},{1,0},{2,3},{3,2},{4,5},{5,4},{6,7},{7,6},{8,9},{9,8},{10,11... | collective-permute-start | bytes 2359304 | tf_op jit(solution)/shard_map/ppermute | solution.py:494
  295.4 3.7 collective-permute-start.20
  (15 other events, 35.9 us)
Sparse Core Ops, SparseCore 0:
  11.4 87.7 all-gather.1

commit v2 on v1

v2 whole, which is shorter than its diff:
```python
import functools

import jax
import jax.numpy as jnp
from jax import lax
from jax.experimental import pallas as pl
from jax.experimental.pallas import tpu as pltpu
from jax.sharding import PartitionSpec as P

F32 = jnp.float32
BF16 = jnp.bfloat16
HEAD_DIM = 64
RANK = 8
LANES = 128
EPS = 1e-05
MASKED = -float(2**30)
SEG = 64
VMEM_LIMIT = 60 * 2**20

NT = (((1,), (1,)), ((), ()))
TN = (((0,), (0,)), ((), ()))


def mm(a, b):
    return jnp.dot(a, b, preferred_element_type=F32)


def mm_nt(a, b):
    return lax.dot_general(a, b, NT, preferred_element_type=F32)


def mm_tn(a, b):
    return lax.dot_general(a, b, TN, preferred_element_type=F32)


def iota(shape, dimension):
    return lax.broadcasted_iota(jnp.int32, shape, dimension)


def three_parts(value, lane):
    high = value.astype(BF16).astype(F32)
    rest = value - high
    middle = rest.astype(BF16).astype(F32)
    return jnp.where(lane < 16, high, jnp.where(lane < 32, middle, jnp.where(lane < 48, rest - middle, 0.0)))


def two_parts(value):
    high = value.astype(BF16)
    return jnp.concatenate([high, (value - high.astype(F32)).astype(BF16)], axis=1)


def weight_copies(layout, offsets, pieces, target, sem, columns):
    copies = []
    for half, first, width, to in columns:
        for ref, blocks in zip(pieces[half], layout, strict=True):
            rows = ref.shape[0] // len(blocks)
            for place, block in enumerate(blocks):
                start = offsets[block]
                if rows % 16 == 0:
                    start = pl.multiple_of(start, 16)
                copies.append(
                    pltpu.make_async_copy(
                        ref.at[pl.ds(place * rows, rows), pl.ds(first, width)],
                        target.at[pl.ds(start, rows), pl.ds(to, width)],
                        sem,
                    )
                )
    return copies


def start_all(copies):
    for copy in copies:
        copy.start()


def wait_all(copies):
    for copy in copies:
        copy.wait()


def places(core, shape, half_slot):
    row = iota(shape, 0)
    return jnp.where(row < half_slot, row + core * half_slot, row - core * half_slot)


def flags_of(core, length, bound, slot):
    lane = iota((slot, LANES), 1)
    place = places(core, (slot, LANES), slot // 2)
    second = place >= bound
    query = jnp.where(
        lane == SEG,
        jnp.where(second, 1.0, 0.0),
        jnp.where(lane == SEG + 1, jnp.where(second, 0.0, 1.0), jnp.where(lane == SEG + 2, 1.0, 0.0)),
    )
    key = jnp.where(
        lane == SEG,
        jnp.where(second, 0.0, MASKED),
        jnp.where(
            lane == SEG + 1,
            jnp.where(second, MASKED, 0.0),
            jnp.where((lane == SEG + 2) & (place >= length), MASKED, 0.0),
        ),
    )
    return lane, query, key


def pair_columns(pair, heads):
    per_half = heads // LANES
    base = (pair // per_half) * 3 * heads + (pair % per_half) * LANES
    return base, base + heads, base + 2 * heads


def load_projections(layout, offsets, pieces, weights, sem, heads, downs):
    wide = 3 * heads
    columns = [(0, 0, wide, 0), (1, 0, wide, wide)]
    columns += [(0, wide, LANES, to) for to in downs]
    return weight_copies(layout, offsets, pieces, weights, sem, columns)


def ups(up_refs, heads):
    blank = jnp.zeros((RANK, heads), BF16)
    parts = []
    for ref in up_refs:
        parts += [
            jnp.concatenate([ref[0] * 2, blank], axis=0),
            jnp.concatenate([blank, blank], axis=0),
            jnp.concatenate([blank, ref[1] * 2], axis=0),
        ]
    return jnp.concatenate(parts, axis=1)


def project_attend_kernel(layout, offsets, lengths, bounds, core_ref, *refs):
    n = len(layout)
    pieces = (refs[:n], refs[n : 2 * n])
    (
        x_own_ref,
        x_got_ref,
        bias_ref,
        up_own_ref,
        up_got_ref,
        qkv_ref,
        mixed_ref,
        spare_ref,
        low_ref,
        weights,
        down,
        sems,
    ) = refs[2 * n :]
    item = pl.program_id(0)
    core = core_ref[0]
    slot, width = mixed_ref.shape[1:]
    heads = width // 2

    @pl.when(item == 0)
    def _():
        wide = 3 * heads
        copies = weight_copies(layout, offsets, pieces, weights, sems.at[0], [(0, 0, wide, 0), (1, 0, wide, wide)])
        downs = weight_copies(layout, offsets, pieces, down, sems.at[1], [(0, wide, LANES, 0)])
        start_all(downs)
        start_all(copies)
        weights[width:] = jnp.zeros((2 * LANES, 6 * heads), BF16)
        up = ups((up_own_ref, up_got_ref), heads)
        weights[width : width + 2 * RANK] = up
        weights[width + LANES : width + LANES + 2 * RANK] = up
        wait_all(downs)
        wait_all(copies)

    x = jnp.concatenate([x_own_ref[0], x_got_ref[0]], axis=0)
    low = two_parts(mm(x, down[...]))
    low_ref[0] = low
    wide_x = jnp.concatenate([x, low], axis=1)
    for part in range(3):
        at = slice(part * width, (part + 1) * width)
        out = (mm(wide_x, weights[:, at]) + bias_ref[0:1, at]) * bias_ref[1:2, at]
        qkv_ref[0, :, at] = out.astype(BF16)

    lane, query_flags, key_flags = flags_of(core, lengths[item], bounds[item], slot)
    query_low = query_flags.astype(BF16)
    key_low = key_flags.astype(BF16)
    ones = jnp.where(lane == 0, 1.0, 0.0).astype(BF16)
    zero = jnp.zeros((slot, LANES), BF16)
    totals = jnp.ones((slot, LANES), F32)
    peaks = []
    for pair in range(width // LANES):
        at_query, at_key, at_value = pair_columns(pair, heads)
        query = qkv_ref[0, :, at_query : at_query + LANES]
        keys = jnp.concatenate([qkv_ref[0, :, at_key : at_key + LANES], key_low], axis=1)
        values = jnp.concatenate([qkv_ref[0, :, at_value : at_value + LANES], ones], axis=1)
        outs = []
        for side in range(2):
            inside = (lane < HEAD_DIM) if side == 0 else (lane >= HEAD_DIM)
            query_side = jnp.concatenate([jnp.where(inside, query, zero), query_low], axis=1)
            scores = mm_nt(keys, query_side)
            peak = jnp.max(scores, axis=0, keepdims=True)
            probs = jnp.exp(scores - peak).astype(BF16)
            out = mm_tn(probs, values)
            total = out[:, LANES : LANES + 1]
            outs.append(out[:, :LANES] * (1.0 / total))
            totals = jnp.where((lane & 15) == 2 * pair + side, total, totals)
            peaks.append(peak)
        mixed_ref[0, :, pair * LANES : (pair + 1) * LANES] = jnp.where(
            lane < HEAD_DIM, outs[0], outs[1]
        ).astype(BF16)
    peaks += [jnp.zeros((1, slot), F32)] * (16 - len(peaks))
    peaks = jnp.concatenate(peaks, axis=0)
    peaks = jnp.concatenate([peaks] * (LANES // 16), axis=0).T
    spare_ref[0] = (three_parts(peaks + jnp.log(totals), lane) + query_flags).astype(BF16)


def row_mean(value):
    return jnp.mean(value, axis=-1, keepdims=True)


def normalize(value):
    centre = value - row_mean(value)
    scale = lax.rsqrt(row_mean(centre * centre) + EPS)
    return centre * scale, scale


def normalize_back(grad, gain, normal, scale):
    grad = grad * gain
    return scale * (grad - row_mean(grad) - normal * row_mean(grad * normal))


def feed_kernel(layouts, chunks, offsets, core_ref, *refs):
    n, m = map(len, layouts)
    pieces = (refs[:n], refs[n : 2 * n])
    pieces_last = (refs[2 * n : 2 * n + m], refs[2 * n + m : 2 * n + 2 * m])
    (
        x_own_ref,
        x_got_ref,
        mixed_ref,
        grad_own_ref,
        grad_got_ref,
        hidden_bias_ref,
        output_bias_ref,
        gain_ref,
        shift_ref,
        out_own_ref,
        out_got_ref,
        grad_hidden_ref,
        grad_mixed_ref,
        out_weights,
        in_weights,
        back_weights,
        slope,
        sems,
    ) = refs[2 * (n + m) :]
    slot, width = mixed_ref.shape[1:]
    half_slot = slot // 2
    heads = width // 2
    first, last = chunks
    parts = [(0, first), (first, first), (2 * first, last), (2 * first + last, last)]

    @pl.when(pl.program_id(0) == 0)
    def _():
        o = heads
        copies = weight_copies(layouts[0], offsets, pieces, out_weights, sems.at[0], [(0, 0, o, 0), (1, 0, o, o)])
        copies += weight_copies(
            layouts[0], offsets, pieces, in_weights, sems.at[0], [(0, o, first, 0), (1, o, first, first)]
        )
        copies += weight_copies(
            layouts[0], offsets, pieces, back_weights, sems.at[0], [(0, o + first, first, 0), (1, o + first, first, first)]
        )
        at = 2 * first
        copies += weight_copies(
            layouts[1], offsets, pieces_last, in_weights, sems.at[0], [(0, 0, last, at), (1, 0, last, at + last)]
        )
        copies += weight_copies(
            layouts[1], offsets, pieces_last, back_weights, sems.at[0], [(0, last, last, at), (1, last, last, at + last)]
        )
        start_all(copies)
        wait_all(copies)

    x = jnp.concatenate([x_own_ref[0], x_got_ref[0]], axis=0).astype(F32)
    summed = x + output_bias_ref[0:1] + mm_nt(mixed_ref[0], out_weights[...])
    normal_in, scale_in = normalize(summed)
    normed = normal_in * gain_ref[0:1] + shift_ref[0:1]
    normed_low = normed.astype(BF16)
    total = normed + output_bias_ref[1:2]
    for at, size in parts:
        pre = mm(normed_low, in_weights[:, at : at + size]) + hidden_bias_ref[:, at : at + size]
        share = 0.5 * (1.0 + lax.erf(pre * 0.7071067811865476))
        slope[:, at : at + size] = share + pre * jnp.exp(-0.5 * pre * pre) * 0.3989422804014327
        total += mm_nt((pre * share).astype(BF16), back_weights[:, at : at + size])
    normal_out, scale_out = normalize(total)
    out = (normal_out * gain_ref[1:2] + shift_ref[1:2]).astype(BF16)
    out_own_ref[0] = out[:half_slot]
    out_got_ref[0] = out[half_slot:]
    grad = jnp.concatenate([grad_own_ref[0], grad_got_ref[0]], axis=0).astype(F32)
    grad_total = normalize_back(grad, gain_ref[1:2], normal_out, scale_out)
    grad_low = grad_total.astype(BF16)
    grad_normed = grad_total
    for at, size in parts:
        grad_pre = (mm(grad_low, back_weights[:, at : at + size]) * slope[:, at : at + size]).astype(BF16)
        grad_normed += mm_nt(grad_pre, in_weights[:, at : at + size])
    grad_hidden = normalize_back(grad_normed, gain_ref[0:1], normal_in, scale_in)
    grad_hidden_ref[0] = grad_hidden
    grad_mixed_ref[0] = mm(grad_hidden.astype(BF16), out_weights[...]).astype(BF16)


def attend_back_kernel(lengths, bounds, core_ref, *refs):
    (
        qkv_ref,
        mixed_ref,
        spare_ref,
        low_ref,
        grad_mixed_ref,
        grads_ref,
        adapter_own_ref,
        adapter_got_ref,
    ) = refs
    item = pl.program_id(0)
    core = core_ref[0]
    slot, width = mixed_ref.shape[1:]
    heads = width // 2

    lane, _, key_flags = flags_of(core, lengths[item], bounds[item], slot)
    row = iota((width, LANES), 0)
    column = iota((width, LANES), 1)
    pick = jnp.where((row // HEAD_DIM == (column & 15)) & (column < 48), 1.0, 0.0).astype(BF16)
    product = grad_mixed_ref[0].astype(F32) * mixed_ref[0].astype(F32)
    high = product.astype(BF16)
    rest = (product - high.astype(F32)).astype(BF16)
    inner = three_parts(mm(high, pick) + mm(rest, pick), lane).astype(BF16)
    spare = spare_ref[0]
    zero = jnp.zeros((slot, LANES), BF16)
    for pair in range(width // LANES):
        at_query, at_key, at_value = pair_columns(pair, heads)
        query = qkv_ref[0, :, at_query : at_query + LANES]
        keys = qkv_ref[0, :, at_key : at_key + LANES]
        values = qkv_ref[0, :, at_value : at_value + LANES]
        grad = grad_mixed_ref[0, :, pair * LANES : (pair + 1) * LANES]
        total_query = jnp.zeros((slot, LANES), F32)
        total_key = jnp.zeros((slot, LANES), F32)
        total_value = jnp.zeros((slot, LANES), F32)
        for side in range(2):
            head = 2 * pair + side
            inside = (lane < HEAD_DIM) if side == 0 else (lane >= HEAD_DIM)
            mine = ((lane & 15) == head) & (lane < 48)
            query_side = jnp.where(inside, query, zero)
            key_side = jnp.where(inside, keys, zero)
            grad_side = jnp.where(inside, grad, zero)
            key_wide = jnp.concatenate([keys, jnp.where(mine, -1.0, key_flags).astype(BF16)], axis=1)
            value_wide = jnp.concatenate([values, jnp.where(mine, -1.0, 0.0).astype(BF16)], axis=1)
            probs = jnp.exp(mm_nt(key_wide, jnp.concatenate([query_side, spare], axis=1)))
            grad_probs = mm_nt(value_wide, jnp.concatenate([grad_side, inner], axis=1))
            grad_scores = (probs * grad_probs).astype(BF16)
            total_value += mm(probs.astype(BF16), grad_side)
            total_key += mm(grad_scores, query_side)
            total_query += mm_tn(grad_scores, key_side)
        grads_ref[0, :, at_query : at_query + LANES] = (total_query * 0.125).astype(BF16)
        grads_ref[0, :, at_key : at_key + LANES] = total_key.astype(BF16)
        grads_ref[0, :, at_value : at_value + LANES] = total_value.astype(BF16)

    update = 2.0 * mm_tn(low_ref[0], grads_ref[0])
    for half, ref in enumerate((adapter_own_ref, adapter_got_ref)):
        at = half * 3 * heads
        of_query = update[:, at : at + heads]
        of_value = update[:, at + 2 * heads : at + 3 * heads]
        part = jnp.concatenate(
            [
                of_query[:RANK] + of_query[LANES : LANES + RANK],
                of_value[RANK : 2 * RANK] + of_value[LANES + RANK : LANES + 2 * RANK],
            ],
            axis=0,
        )

        @pl.when(item == 0)
        def _(ref=ref, part=part):
            ref[...] = part

        @pl.when(item > 0)
        def _(ref=ref, part=part):
            ref[...] += part


def input_grad_kernel(layout, offsets, core_ref, *refs):
    n = len(layout)
    pieces = (refs[:n], refs[n : 2 * n])
    (
        grads_ref,
        grad_hidden_ref,
        up_own_ref,
        up_got_ref,
        own_ref,
        got_ref,
        weights,
        up,
        sems,
    ) = refs[2 * n :]
    slot, width = grad_hidden_ref.shape[1:]
    heads = width // 2

    @pl.when(pl.program_id(0) == 0)
    def _():
        copies = load_projections(layout, offsets, pieces, weights, sems.at[0], heads, (6 * heads, 6 * heads + LANES))
        start_all(copies)
        up[...] = jnp.zeros_like(up)
        up[: 2 * RANK] = ups((up_own_ref, up_got_ref), heads)
        wait_all(copies)

    grads = grads_ref[0]
    small = two_parts(mm_nt(grads, up[...]))
    total = grad_hidden_ref[0] + mm_nt(jnp.concatenate([grads, small], axis=1), weights[...])
    own_ref[0] = total[: slot // 2]
    got_ref[0] = total[slot // 2 :]


def any_spec():
    return pl.BlockSpec(memory_space=pl.ANY)


def whole_spec(array):
    return pl.BlockSpec(array.shape, lambda i, *_: (0,) * array.ndim)


def item_spec(shape):
    return pl.BlockSpec((1, *shape[1:]), lambda i, *_: (i, 0, 0))


def shape_of(shape, dtype):
    return jax.ShapeDtypeStruct(shape, dtype)


def call(kernel, name, scalars, flat, args, outs, scratch, items, flops, moved):
    return pl.pallas_call(
        kernel,
        grid_spec=pltpu.PrefetchScalarGridSpec(
            num_scalar_prefetch=len(scalars),
            grid=(items,),
            in_specs=[any_spec()] * len(flat) + [spec for _, spec in args],
            out_specs=[spec for _, spec in outs],
            scratch_shapes=scratch,
        ),
        out_shape=[shape for shape, _ in outs],
        compiler_params=pltpu.CompilerParams(vmem_limit_bytes=VMEM_LIMIT),
        cost_estimate=pl.CostEstimate(flops=flops, bytes_accessed=moved, transcendentals=0),
        name=name,
    )(*scalars, *flat, *[array for array, _ in args])


def swap(array):
    return lax.ppermute(array, "tensor", [(0, 1), (1, 0)])


def after(value, *deps):
    return lax.optimization_barrier((value, *deps))[0]


def over_dp(count, array, target):
    return lax.ppermute(array, "dp", [(i, target(i)) for i in range(count)])


LINE_FIRST = ((0, 1, 2, 3), (4, 5, 6, 7), (8, 9, 10, 11), (12, 13), (14, 15))
PLANE_FIRST = ((0, 4, 8, 12), (1, 5, 9, 13), (2, 6, 10, 14), (3, 7, 11, 15))


def ring_offsets(index, rows):
    flip = jnp.arange(16) // 4
    back = jnp.arange(16) % 4
    return (((index ^ flip) - 4 * back) % 16 * rows).astype(jnp.int32)


def local(
    inputs,
    lengths,
    bounds,
    query_matrix,
    key_matrix,
    value_matrix,
    query_value_bias,
    adapter_down_weight,
    adapter_up_weight,
    attention_output_weight,
    feedforward_input_weight,
    feedforward_input_bias,
    feedforward_output_weight,
    output_bias,
    layernorm_scale,
    layernorm_bias,
    output_gradient,
    *,
    count,
):
    micro, rows, width = inputs.shape
    mine = micro // 2
    slot = 2 * rows
    heads = width // 2
    core = lax.axis_index("tensor")
    shard_rows = query_matrix.shape[0]
    hidden = feedforward_input_weight.shape[1]
    last = hidden // 3
    first = hidden - last

    down = jnp.transpose(adapter_down_weight, (1, 0, 2)).reshape(shard_rows, 2 * RANK)
    down = jnp.pad(down, ((0, 0), (0, LANES - 2 * RANK)))
    shard = jnp.concatenate([query_matrix, key_matrix, value_matrix, down], axis=1)
    back = feedforward_output_weight.T
    shard_first = jnp.concatenate(
        [attention_output_weight.T, feedforward_input_weight[:, :first], back[:, :first]], axis=1
    )
    shard_last = jnp.concatenate([feedforward_input_weight[:, first:], back[:, first:]], axis=1)

    others = (1 - core) * mine
    x_got = swap(lax.dynamic_slice_in_dim(inputs, others, mine, 0))
    grad_got = swap(lax.dynamic_slice_in_dim(output_gradient, others, mine, 0))
    bias_got, hidden_bias_got, up_got = swap(query_value_bias), swap(feedforward_input_bias), swap(adapter_up_weight)

    if count == 16:
        offsets = ring_offsets(lax.axis_index("dp"), shard_rows)
        move = functools.partial(over_dp, count)

        def to_x(array):
            return move(array, lambda i: i ^ 1)

        def to_y(array):
            return move(array, lambda i: i ^ 2)

        def along_z(array):
            return [array] + [move(array, lambda i, d=d: (i + 4 * d) % 16) for d in (1, 2, 3)]

        def far(by_x, by_y):
            half = by_x.shape[0] // 2
            return [to_y(by_x[:half]), to_x(by_y[half:])]

        plane = [shard_last, to_x(shard_last), to_y(shard_last), move(shard_last, lambda i: i ^ 3)]
        line = jnp.concatenate(along_z(shard), axis=0)
        plane = jnp.concatenate(plane, axis=0)
        shard_first, plane = lax.optimization_barrier((shard_first, plane, line))[:2]
        near = [to_x(line), to_y(line)]
        line_first = jnp.concatenate(along_z(shard_first), axis=0)
        own = [line, *near, *far(*near)]
        line_first, plane = lax.optimization_barrier((line_first, plane, own[3], own[4]))[:2]
        own_last = along_z(plane)
        near_first = [to_x(line_first), to_y(line_first)]
        own_first = [line_first, *near_first, *far(*near_first)]
        layout, layout_last = LINE_FIRST, PLANE_FIRST
    else:
        offsets = jnp.zeros((2,), jnp.int32)
        layout = layout_last = ((0,),)
        own, own_first, own_last = (
            [lax.all_gather(s, "dp", axis=0, tiled=True)] for s in (shard, shard_first, shard_last)
        )
    pieces = (*own, *map(swap, own))
    pieces_feed = (*own_first, *map(swap, own_first), *own_last, *map(swap, own_last))

    first_item = core * mine
    my_lengths = lax.dynamic_slice_in_dim(lengths[:, 0], first_item, mine, 0)
    my_bounds = lax.dynamic_slice_in_dim(bounds[:, 0], first_item, mine, 0)
    core = core[None].astype(jnp.int32)

    blank = jnp.zeros((heads,), F32)
    ones = blank + 1
    both = [query_value_bias[0], blank, query_value_bias[1], bias_got[0], blank, bias_got[1]]
    scale = [ones * 0.125, ones, ones] * 2
    bias = jnp.stack([jnp.concatenate(both), jnp.concatenate(scale)])
    hidden_bias = jnp.concatenate(
        [
            feedforward_input_bias[:first],
            hidden_bias_got[:first],
            feedforward_input_bias[first:],
            hidden_bias_got[first:],
        ]
    )[None]

    own_block = pl.BlockSpec((1, rows, width), lambda i, *s: (s[-1][0] * mine + i, 0, 0))
    got_block = pl.BlockSpec((1, rows, width), lambda i, *_: (i, 0, 0))
    item = (mine, slot, width)
    wide = (mine, slot, 3 * width)

    def out_item(shape, dtype):
        return shape_of(shape, dtype), item_spec(shape)

    def in_item(array):
        return array, item_spec(array.shape)

    def in_whole(array):
        return array, whole_spec(array)

    split_out = lambda dtype: [(shape_of(inputs.shape, dtype), own_block), (shape_of((mine, rows, width), dtype), got_block)]

    tokens = mine * slot
    qkv, mixed, spare, low = call(
        functools.partial(project_attend_kernel, layout),
        "project_attend",
        (offsets, my_lengths, my_bounds, core),
        pieces,
        [(inputs, own_block), (x_got, got_block), in_whole(bias), in_whole(adapter_up_weight), in_whole(up_got)],
        [
            out_item(wide, BF16),
            out_item(item, BF16),
            out_item((mine, slot, LANES), BF16),
            out_item((mine, slot, 2 * LANES), BF16),
        ],
        [
            pltpu.VMEM((width + 2 * LANES, 3 * width), BF16),
            pltpu.VMEM((width, LANES), BF16),
            pltpu.SemaphoreType.DMA((2,)),
        ],
        mine,
        2 * tokens * width * (4 * width + 8 * slot),
        12 * tokens * width,
    )
    out, out_send, grad_hidden, grad_mixed = call(
        functools.partial(feed_kernel, (layout, layout_last), (first, last)),
        "feed",
        (offsets, core),
        pieces_feed,
        [
            (inputs, own_block),
            (x_got, got_block),
            in_item(mixed),
            (output_gradient, own_block),
            (grad_got, got_block),
            *map(in_whole, (hidden_bias, output_bias, layernorm_scale, layernorm_bias)),
        ],
        [*split_out(BF16), out_item(item, F32), out_item(item, BF16)],
        [
            pltpu.VMEM((width, width), BF16),
            pltpu.VMEM((width, 2 * hidden), BF16),
            pltpu.VMEM((width, 2 * hidden), BF16),
            pltpu.VMEM((slot, 2 * hidden), F32),
            pltpu.SemaphoreType.DMA((1,)),
        ],
        mine,
        4 * tokens * width * (width + 4 * hidden),
        8 * width * hidden,
    )
    adapter = (2 * RANK, heads)
    grads, adapter_own, adapter_got = call(
        attend_back_kernel,
        "attend_back",
        (my_lengths, my_bounds, core),
        (),
        [*map(in_item, (qkv, mixed, spare, low, grad_mixed))],
        [out_item(wide, BF16)] + [(shape_of(adapter, F32), pl.BlockSpec(adapter, lambda i, *_: (0, 0)))] * 2,
        [],
        mine,
        2 * tokens * width * 20 * slot,
        16 * tokens * width,
    )
    total, total_send = call(
        functools.partial(input_grad_kernel, layout),
        "input_grad",
        (offsets, core),
        pieces,
        [in_item(grads), in_item(grad_hidden), in_whole(adapter_up_weight), in_whole(up_got)],
        split_out(F32),
        [
            pltpu.VMEM((width, 3 * width + 2 * LANES), BF16),
            pltpu.VMEM((LANES, 3 * width), BF16),
            pltpu.SemaphoreType.DMA((1,)),
        ],
        mine,
        2 * tokens * width * 3 * width,
        12 * tokens * width,
    )
    adapter = adapter_own + swap(adapter_got)
    if count == 16:
        for step in (1, 2, 4, 8):
            adapter = adapter + over_dp(count, adapter, lambda i, step=step: i ^ step)
    else:
        adapter = lax.psum(adapter, "dp")
    result = lax.dynamic_update_slice_in_dim(out, swap(out_send), others, 0)
    input_grad = lax.dynamic_update_slice_in_dim(total, swap(total_send), others, 0)
    return result, input_grad, adapter.reshape(2, RANK, heads)


def solution(mesh):
    return jax.shard_map(
        functools.partial(local, count=mesh.shape["dp"]),
        mesh=mesh,
        in_specs=(
            P(None, ("dp", "tensor"), None),
            P(None, "dp"),
            P(None, "dp"),
            P("dp", "tensor"),
            P("dp", "tensor"),
            P("dp", "tensor"),
            P(None, "tensor"),
            P(None, "dp", None),
            P(None, None, "tensor"),
            P("tensor", "dp"),
            P("dp", "tensor"),
            P("tensor"),
            P("tensor", "dp"),
            P(),
            P(),
            P(),
            P(None, ("dp", "tensor"), None),
        ),
        out_specs=(
            P(None, ("dp", "tensor"), None),
            P(None, ("dp", "tensor"), None),
            P(None, None, "tensor"),
        ),
        check_vma=False,
    )
```

time: 383 us -> 214 us (0.56); the launches traced: 386 us -> 211 us
  blocking collectives: 73.6 us -> 0 us
  waiting for transfers between devices: 126 us -> 64 us
  Pallas kernels: 133 us -> 94.1 us
  starting transfers between devices: 11.7 us -> 33.7 us
  other arithmetic: 19.3 us -> 5.02 us
  between operations: 14.5 us -> 1.66 us
  local copies, waits for them, and re-layouts: 8.58 us -> 12.5 us
    all_gather x1 -> x0, waiting for transfers between devices: 90.1 us -> none  [local(): own_feed = [lax.all_gather(shard_feed, 'dp', axis=0, tiled=True)]]
    psum x1 -> x0, blocking collectives: 73.6 us -> none  [local(): adapter = lax.psum(adapter, 'dp').reshape(2, RANK, half)]
    pallas_call x3 -> x4, Pallas kernels: 133 us -> 94.1 us  [call(): pl.pallas_call(kernel, grid_spec=pltpu.PrefetchScalarGridSpec(num_scalar_...]
    ppermute x7 -> x24, waiting for transfers between devices: 27.9 us -> 59.4 us  [over_dp(): return lax.ppermute(array, 'dp', [(i, target(i)) for i in range(count)])]
    ppermute x7 -> x24, starting transfers between devices: 9.16 us -> 29.3 us  [over_dp(): return lax.ppermute(array, 'dp', [(i, target(i)) for i in range(count)])]
    select_n x4 -> x0, other arithmetic: 12.8 us -> none  [the longest x2 6.64 us: give_items(): jnp.where(core == 0, jnp.concatenate([kept, got], axis=0), jnp.concatenat...]
    slice x3 -> x15, local copies, waits for them, and re-layouts: 0.98 us -> 5.65 us  [the longest x4 3.09 us: far(): return [to_y(by_x[:half]), to_x(by_y[half:])]]
  transfers between devices with their start and end apart: 22 -> 46, of which waited for: 10 -> 12; matrix products, arithmetic and copies ran while one was open for 4% -> 5% of each run, Pallas kernels for 9% -> 10%
where the time goes in v2:
time: 214 us; the launch traced here: 211 us
  Pallas kernels  94.1 us (44%)
  waiting for transfers between devices  64 us (30%)
  starting transfers between devices  33.7 us (16%)
  local copies, waits for them, and re-layouts  12.5 us (6%)
  other arithmetic  5.02 us (2%)
    pallas_call x4, Pallas kernels, call(): pl.pallas_call(kernel, grid_spec=pltpu.PrefetchScalarGridSpec(num_scalar_...  94.1 us
    ppermute x24, waiting for transfers between devices, over_dp(): return lax.ppermute(array, 'dp', [(i, target(i)) for i in range(count)])  59.4 us
    ppermute x24, starting transfers between devices, over_dp(): return lax.ppermute(array, 'dp', [(i, target(i)) for i in range(count)])  29.3 us
    ppermute x22, waiting for transfers between devices, swap(): return lax.ppermute(array, 'tensor', [(0, 1), (1, 0)])  4.63 us
    ppermute x22, starting transfers between devices, swap(): return lax.ppermute(array, 'tensor', [(0, 1), (1, 0)])  4.41 us
  transfers between devices with their start and end apart: 46, of which 12 were waited for; matrix products, arithmetic and copies ran while one was open for 5% of the time, Pallas kernels for 10%

profile of v2, /device:TPU:0, one launch (start us, length us, event | category | flops | bytes accessed | tf_op | source)
XLA Modules:
  0.0 211.0 jit_solution(14289053615737572791)
XLA Ops:
  2.3 5.1 %collective-permute-start.5 = (bf16[48,1280]{1,0:T(8,128)(2,1)S(1)}, bf16[48,1280]{1,0:T(8,128)(2,1)S(1)}, u32[]{:S(2)}, u32[]{:S(2)}) collective-permute-start(bf16[48,1280]{1,0:T(8,128)(2,1)S(1)} %pad_maximum_fusion.4), channel_id=1, source_target_pairs={{0,24},{2,26},{4,28},{6,30},{8,0},{10,2},{12,4},{14,6},{16,8},{18,... | collective-permute-start | bytes 368648 | tf_op jit(solution)/shard_map/ppermute | solution.py:452
  10.1 2.5 %collective-permute-start.2 = (bf16[48,1024]{1,0:T(8,128)(2,1)S(1)}, bf16[48,1024]{1,0:T(8,128)(2,1)S(1)}, u32[]{:S(2)}, u32[]{:S(2)}) collective-permute-start(bf16[48,1024]{1,0:T(8,128)(2,1)S(1)} %pad_maximum_fusion.5), channel_id=1, source_target_pairs={{0,6},{2,4},{4,2},{6,0},{8,14},{10,12},{12,10},{14,8},{16,22},{18,... | collective-permute-start | bytes 294920 | tf_op jit(solution)/shard_map/ppermute | solution.py:452
  14.6 3.4 %collective-permute-done.4 = bf16[48,1280]{1,0:T(8,128)(2,1)S(1)} collective-permute-done((bf16[48,1280]{1,0:T(8,128)(2,1)S(1)}, bf16[48,1280]{1,0:T(8,128)(2,1)S(1)}, u32[]{:S(2)}, u32[]{:S(2)}) %collective-permute-start.4) | collective-permute-done | bytes 122912 | tf_op jit(solution)/shard_map/ppermute | solution.py:452
  18.9 1.6 collective-permute-start.11
  20.5 1.5 collective-permute-start.9
  22.8 1.6 collective-permute-start.8
  25.5 6.2 %collective-permute-done.11.refs_2_ = bf16[192,1280]{1,0:T(8,128)(2,1)} collective-permute-done((bf16[192,1280]{1,0:T(8,128)(2,1)S(1)}, bf16[192,1280]{1,0:T(8,128)(2,1)}, u32[]{:S(2)}, u32[]{:S(2)}) %collective-permute-start.11) | collective-permute-done | bytes 491552 | tf_op jit(solution)/shard_map/ppermute | solution.py:452
  33.1 1.6 collective-permute-start.12
  34.7 1.6 collective-permute-start.10
  36.6 8.4 %collective-permute-done.7 = bf16[48,2432]{1,0:T(8,128)(2,1)S(1)} collective-permute-done((bf16[48,2432]{1,0:T(8,128)(2,1)S(1)}, bf16[48,2432]{1,0:T(8,128)(2,1)S(1)}, u32[]{:S(2)}, u32[]{:S(2)}) %collective-permute-start.7) | collective-permute-done | bytes 233504 | tf_op jit(solution)/shard_map/ppermute | solution.py:452
  53.2 17.1 %collective-permute-done.14.refs_2_ = bf16[192,2432]{1,0:T(8,128)(2,1)} collective-permute-done((bf16[192,2432]{1,0:T(8,128)(2,1)S(1)}, bf16[192,2432]{1,0:T(8,128)(2,1)}, u32[]{:S(2)}, u32[]{:S(2)}) %collective-permute-start.14) | collective-permute-done | bytes 933920 | tf_op jit(solution)/shard_map/ppermute | solution.py:452
  73.3 1.5 collective-permute-start.15
  74.9 13.1 %collective-permute-done.23.refs_12_ = bf16[192,1024]{1,0:T(8,128)(2,1)S(1)} collective-permute-done((bf16[192,1024]{1,0:T(8,128)(2,1)}, bf16[192,1024]{1,0:T(8,128)(2,1)S(1)}, u32[]{:S(2)}, u32[]{:S(2)}) %collective-permute-start.23) | collective-permute-done | bytes 393248 | tf_op jit(solution)/shard_map/ppermute | solution.py:452
  91.3 21.7 %project_attend.1 = (bf16[2,512,2304]{2,1,0:T(8,128)(2,1)}, bf16[2,512,768]{2,1,0:T(8,128)(2,1)}, bf16[2,512,128]{2,1,0:T(8,128)(2,1)}, bf16[2,512,256]{2,1,0:T(8,128)(2,1)}) custom-call(s32[16]{0:T(128)} %fusion.5.offsets, s32[2]{0:T(128)} %get-tuple-element.41.lengths, s32[2]{0:T(128)} %get-tuple-element.42.bounds, s32[1]{0:T(128)} %bitcast.core_ref, ...), custom_call_target="tpu_custom_call" | custom-call | flops 11274289152 | bytes 9437184 | tf_op jit(solution)/shard_map/project_attend/pallas_call | solution.py:427
  114.4 36.4 %feed.1 = (bf16[4,256,768]{2,1,0:T(8,128)(2,1)}, bf16[2,256,768]{2,1,0:T(8,128)(2,1)}, f32[2,512,768]{2,1,0:T(8,128)}, bf16[2,512,768]{2,1,0:T(8,128)(2,1)}) custom-call(s32[16]{0:T(128)} %fusion.5.offsets, s32[1]{0:T(128)} %bitcast.core_ref, bf16[192,2432]{1,0:T(8,128)(2,1)} %copy-done, bf16[192,2432]{1,0:T(8,128)(2,1)} %collective-permute-done.13.refs_1_, ...), custom_call_target="tpu_custom_call" | custom-call | flops 21743271936 | bytes 9437184 | tf_op jit(solution)/shard_map/feed/pallas_call | solution.py:427
  150.8 23.9 %attend_back.1 = (bf16[2,512,2304]{2,1,0:T(8,128)(2,1)}, f32[16,384]{1,0:T(8,128)}, f32[16,384]{1,0:T(8,128)}) custom-call(s32[2]{0:T(128)} %get-tuple-element.41.lengths, s32[2]{0:T(128)} %get-tuple-element.42.bounds, s32[1]{0:T(128)} %bitcast.core_ref, bf16[2,512,2304]{2,1,0:T(8,128)(2,1)} %get-tuple-element.27.refs_0_, ...), custom_call_target="tpu_custom_call" | custom-call | flops 16106127360 | bytes 12582912 | tf_op jit(solution)/shard_map/attend_back/pallas_call | solution.py:427
  174.8 12.1 %input_grad.1 = (f32[4,256,768]{2,1,0:T(8,128)}, f32[2,256,768]{2,1,0:T(8,128)}) custom-call(s32[16]{0:T(128)} %fusion.5.offsets, s32[1]{0:T(128)} %bitcast.core_ref, bf16[192,1280]{1,0:T(8,128)(2,1)} %copy-done.1, bf16[192,1280]{1,0:T(8,128)(2,1)} %copy-done.4, bf16[192,1280]{1,0:T(8,128)(2,1)} %collective-permute-done.11.refs_2_, ...), custom_call_target="tpu_custom_call" | custom-call | flops 3623878656 | bytes 9437184 | tf_op jit(solution)/shard_map/input_grad/pallas_call | solution.py:427
  187.7 4.0 %collective-permute-done.41 = f32[16,384]{1,0:T(8,128)S(1)} collective-permute-done((f32[16,384]{1,0:T(8,128)S(1)}, f32[16,384]{1,0:T(8,128)S(1)}, u32[]{:S(2)}, u32[]{:S(2)}) %collective-permute-start.41) | collective-permute-done | bytes 24608 | tf_op jit(solution)/shard_map/ppermute | solution.py:444
  193.0 2.6 %collective-permute-done.42 = f32[16,384]{1,0:T(8,128)S(1)} collective-permute-done((f32[16,384]{1,0:T(8,128)S(1)}, f32[16,384]{1,0:T(8,128)S(1)}, u32[]{:S(2)}, u32[]{:S(2)}) %collective-permute-start.42) | collective-permute-done | bytes 24608 | tf_op jit(solution)/shard_map/ppermute | solution.py:452
  196.8 2.6 %collective-permute-done.43 = f32[16,384]{1,0:T(8,128)S(1)} collective-permute-done((f32[16,384]{1,0:T(8,128)S(1)}, f32[16,384]{1,0:T(8,128)S(1)}, u32[]{:S(2)}, u32[]{:S(2)}) %collective-permute-start.43) | collective-permute-done | bytes 24608 | tf_op jit(solution)/shard_map/ppermute | solution.py:452
  199.9 3.3 %collective-permute-done.44 = f32[16,384]{1,0:T(8,128)S(1)} collective-permute-done((f32[16,384]{1,0:T(8,128)S(1)}, f32[16,384]{1,0:T(8,128)S(1)}, u32[]{:S(2)}, u32[]{:S(2)}) %collective-permute-start.44) | collective-permute-done | bytes 24608 | tf_op jit(solution)/shard_map/ppermute | solution.py:452
  203.3 2.4 %collective-permute-start.45 = (f32[16,384]{1,0:T(8,128)S(1)}, f32[16,384]{1,0:T(8,128)S(1)}, u32[]{:S(2)}, u32[]{:S(2)}) collective-permute-start(f32[16,384]{1,0:T(8,128)S(1)} %add.45), channel_id=1, source_target_pairs={{0,16},{2,18},{4,20},{6,22},{8,24},{10,26},{12,28},{14,30},{16,0},... | collective-permute-start | bytes 73736 | tf_op jit(solution)/shard_map/ppermute | solution.py:452
  205.6 2.6 %collective-permute-done.45 = f32[16,384]{1,0:T(8,128)S(1)} collective-permute-done((f32[16,384]{1,0:T(8,128)S(1)}, f32[16,384]{1,0:T(8,128)S(1)}, u32[]{:S(2)}, u32[]{:S(2)}) %collective-permute-start.45) | collective-permute-done | bytes 24608 | tf_op jit(solution)/shard_map/ppermute | solution.py:452
  208.9 1.3 constant_dynamic-update-slice_fusion.6
  (188 shorter events, 31.3 us)
Async XLA Ops:
  10.1 11.9 %collective-permute-start.2 = (bf16[48,1024]{1,0:T(8,128)(2,1)S(1)}, bf16[48,1024]{1,0:T(8,128)(2,1)S(1)}, u32[]{:S(2)}, u32[]{:S(2)}) collective-permute-start(bf16[48,1024]{1,0:T(8,128)(2,1)S(1)} %pad_maximum_fusion.5), channel_id=1, source_target_pairs={{0,6},{2,4},{4,2},{6,0},{8,14},{10,12},{12,10},{14,8},{16,22},{18,... | collective-permute-start | bytes 294920 | tf_op jit(solution)/shard_map/ppermute | solution.py:452
  18.9 12.7 %collective-permute-start.11 = (bf16[192,1280]{1,0:T(8,128)(2,1)S(1)}, bf16[192,1280]{1,0:T(8,128)(2,1)}, u32[]{:S(2)}, u32[]{:S(2)}) collective-permute-start(bf16[192,1280]{1,0:T(8,128)(2,1)S(1)} %pad_maximum_fusion.1.refs_0_), channel_id=1, source_target_pairs={{0,4},{2,6},{4,0},{6,2},{8,12},{10,14},{12,8},{14,10},{16,20},{18,... | collective-permute-start | bytes 1474568 | tf_op jit(solution)/shard_map/ppermute | solution.py:452
  20.5 12.6 %collective-permute-start.9 = (bf16[192,1280]{1,0:T(8,128)(2,1)S(1)}, bf16[192,1280]{1,0:T(8,128)(2,1)S(1)}, u32[]{:S(2)}, u32[]{:S(2)}) collective-permute-start(bf16[192,1280]{1,0:T(8,128)(2,1)S(1)} %pad_maximum_fusion.1.refs_0_), channel_id=1, source_target_pairs={{0,2},{2,0},{4,6},{6,4},{8,10},{10,8},{12,14},{14,12},{16,18},{18,... | collective-permute-start | bytes 1474568 | tf_op jit(solution)/shard_map/ppermute | solution.py:452
  22.8 13.5 %collective-permute-start.8 = (bf16[48,2432]{1,0:T(8,128)(2,1)S(1)}, bf16[48,2432]{1,0:T(8,128)(2,1)S(1)}, u32[]{:S(2)}, u32[]{:S(2)}) collective-permute-start(bf16[48,2432]{1,0:T(8,128)(2,1)S(1)} %pad_maximum_fusion.3), channel_id=1, source_target_pairs={{0,24},{2,26},{4,28},{6,30},{8,0},{10,2},{12,4},{14,6},{16,8},{18,... | collective-permute-start | bytes 700424 | tf_op jit(solution)/shard_map/ppermute | solution.py:452
  24.5 20.5 %collective-permute-start.7 = (bf16[48,2432]{1,0:T(8,128)(2,1)S(1)}, bf16[48,2432]{1,0:T(8,128)(2,1)S(1)}, u32[]{:S(2)}, u32[]{:S(2)}) collective-permute-start(bf16[48,2432]{1,0:T(8,128)(2,1)S(1)} %pad_maximum_fusion.3), channel_id=1, source_target_pairs={{0,16},{2,18},{4,20},{6,22},{8,24},{10,26},{12,28},{14,30},{16,0},... | collective-permute-start | bytes 700424 | tf_op jit(solution)/shard_map/ppermute | solution.py:452
  31.6 13.3 %collective-permute-start.6 = (bf16[48,2432]{1,0:T(8,128)(2,1)S(1)}, bf16[48,2432]{1,0:T(8,128)(2,1)S(1)}, u32[]{:S(2)}, u32[]{:S(2)}) collective-permute-start(bf16[48,2432]{1,0:T(8,128)(2,1)S(1)} %pad_maximum_fusion.3), channel_id=1, source_target_pairs={{0,8},{2,10},{4,12},{6,14},{8,16},{10,18},{12,20},{14,22},{16,24},... | collective-permute-start | bytes 700424 | tf_op jit(solution)/shard_map/ppermute | solution.py:452
  33.1 12.4 %collective-permute-start.12 = (bf16[96,1280]{1,0:T(8,128)(2,1)S(1)}, bf16[96,1280]{1,0:T(8,128)(2,1)S(1)}, u32[]{:S(2)}, u32[]{:S(2)}) collective-permute-start(bf16[96,1280]{1,0:T(8,128)(2,1)S(1)} %slice.67), channel_id=1, source_target_pairs={{0,2},{2,0},{4,6},{6,4},{8,10},{10,8},{12,14},{14,12},{16,18},{18,... | collective-permute-start | bytes 737288 | tf_op jit(solution)/shard_map/ppermute | solution.py:452
  36.4 13.2 %collective-permute-start.29 = (bf16[2,256,768]{2,1,0:T(8,128)(2,1)S(1)}, bf16[2,256,768]{2,1,0:T(8,128)(2,1)}, u32[]{:S(2)}, u32[]{:S(2)}) collective-permute-start(bf16[2,256,768]{2,1,0:T(8,128)(2,1)S(1)} %constant_dynamic-slice_fusion.3), channel_id=1, source_target_pairs={{0,1},{1,0},{2,3},{3,2},{4,5},{5,4},{6,7},{7,6},{8,9},{9,8},{10,11... | collective-permute-start | bytes 2359304 | tf_op jit(solution)/shard_map/ppermute | solution.py:444
  47.0 23.2 %collective-permute-start.14 = (bf16[192,2432]{1,0:T(8,128)(2,1)S(1)}, bf16[192,2432]{1,0:T(8,128)(2,1)}, u32[]{:S(2)}, u32[]{:S(2)}) collective-permute-start(bf16[192,2432]{1,0:T(8,128)(2,1)S(1)} %pad_maximum_fusion.refs_0_), channel_id=1, source_target_pairs={{0,4},{2,6},{4,0},{6,2},{8,12},{10,14},{12,8},{14,10},{16,20},{18,... | collective-permute-start | bytes 2801672 | tf_op jit(solution)/shard_map/ppermute | solution.py:452
  47.6 22.9 %collective-permute-start.13 = (bf16[192,2432]{1,0:T(8,128)(2,1)S(1)}, bf16[192,2432]{1,0:T(8,128)(2,1)}, u32[]{:S(2)}, u32[]{:S(2)}) collective-permute-start(bf16[192,2432]{1,0:T(8,128)(2,1)S(1)} %pad_maximum_fusion.refs_0_), channel_id=1, source_target_pairs={{0,2},{2,0},{4,6},{6,4},{8,10},{10,8},{12,14},{14,12},{16,18},{18,... | collective-permute-start | bytes 2801672 | tf_op jit(solution)/shard_map/ppermute | solution.py:452
  50.9 22.5 %collective-permute-start.25 = (bf16[192,1024]{1,0:T(8,128)(2,1)}, bf16[192,1024]{1,0:T(8,128)(2,1)S(1)}, u32[]{:S(2)}, u32[]{:S(2)}) collective-permute-start(bf16[192,1024]{1,0:T(8,128)(2,1)} %pad_maximum_fusion.2.refs_10_), channel_id=1, source_target_pairs={{0,1},{1,0},{2,3},{3,2},{4,5},{5,4},{6,7},{7,6},{8,9},{9,8},{10,11... | collective-permute-start | bytes 1179656 | tf_op jit(solution)/shard_map/ppermute | solution.py:444
  51.7 23.1 %collective-permute-start.24 = (bf16[192,1024]{1,0:T(8,128)(2,1)}, bf16[192,1024]{1,0:T(8,128)(2,1)S(1)}, u32[]{:S(2)}, u32[]{:S(2)}) collective-permute-start(bf16[192,1024]{1,0:T(8,128)(2,1)} %pad_maximum_fusion.2.refs_10_), channel_id=1, source_target_pairs={{0,24},{2,26},{4,28},{6,30},{8,0},{10,2},{12,4},{14,6},{16,8},{18,... | collective-permute-start | bytes 1179656 | tf_op jit(solution)/shard_map/ppermute | solution.py:452
  52.7 35.3 %collective-permute-start.23 = (bf16[192,1024]{1,0:T(8,128)(2,1)}, bf16[192,1024]{1,0:T(8,128)(2,1)S(1)}, u32[]{:S(2)}, u32[]{:S(2)}) collective-permute-start(bf16[192,1024]{1,0:T(8,128)(2,1)} %pad_maximum_fusion.2.refs_10_), channel_id=1, source_target_pairs={{0,16},{2,18},{4,20},{6,22},{8,24},{10,26},{12,28},{14,30},{16,0},... | collective-permute-start | bytes 1179656 | tf_op jit(solution)/shard_map/ppermute | solution.py:452
  70.3 17.8 %collective-permute-start.22 = (bf16[192,1024]{1,0:T(8,128)(2,1)}, bf16[192,1024]{1,0:T(8,128)(2,1)S(1)}, u32[]{:S(2)}, u32[]{:S(2)}) collective-permute-start(bf16[192,1024]{1,0:T(8,128)(2,1)} %pad_maximum_fusion.2.refs_10_), channel_id=1, source_target_pairs={{0,8},{2,10},{4,12},{6,14},{8,16},{10,18},{12,20},{14,22},{16,24},... | collective-permute-start | bytes 1179656 | tf_op jit(solution)/shard_map/ppermute | solution.py:452
  72.7 17.9 %collective-permute-start.16 = (bf16[96,2432]{1,0:T(8,128)(2,1)S(1)}, bf16[96,2432]{1,0:T(8,128)(2,1)S(1)}, u32[]{:S(2)}, u32[]{:S(2)}) collective-permute-start(bf16[96,2432]{1,0:T(8,128)(2,1)S(1)} %slice.69), channel_id=1, source_target_pairs={{0,2},{2,0},{4,6},{6,4},{8,10},{10,8},{12,14},{14,12},{16,18},{18,... | collective-permute-start | bytes 1400840 | tf_op jit(solution)/shard_map/ppermute | solution.py:452
  73.3 17.7 %collective-permute-start.15 = (bf16[96,2432]{1,0:T(8,128)(2,1)S(1)}, bf16[96,2432]{1,0:T(8,128)(2,1)}, u32[]{:S(2)}, u32[]{:S(2)}) collective-permute-start(bf16[96,2432]{1,0:T(8,128)(2,1)S(1)} %slice.68), channel_id=1, source_target_pairs={{0,4},{2,6},{4,0},{6,2},{8,12},{10,14},{12,8},{14,10},{16,20},{18,... | collective-permute-start | bytes 1400840 | tf_op jit(solution)/shard_map/ppermute | solution.py:452
  74.8 14.9 %collective-permute-start.28 = (bf16[192,1024]{1,0:T(8,128)(2,1)S(1)}, bf16[192,1024]{1,0:T(8,128)(2,1)S(1)}, u32[]{:S(2)}, u32[]{:S(2)}) collective-permute-start(bf16[192,1024]{1,0:T(8,128)(2,1)S(1)} %collective-permute-done.24.refs_13_), channel_id=1, source_target_pairs={{0,1},{1,0},{2,3},{3,2},{4,5},{5,4},{6,7},{7,6},{8,9},{9,8},{10,11... | collective-permute-start | bytes 1179656 | tf_op jit(solution)/shard_map/ppermute | solution.py:444
  89.8 23.2 %collective-permute-start.17 = (bf16[192,2432]{1,0:T(8,128)(2,1)S(1)}, bf16[192,2432]{1,0:T(8,128)(2,1)S(1)}, u32[]{:S(2)}, u32[]{:S(2)}) collective-permute-start(bf16[192,2432]{1,0:T(8,128)(2,1)S(1)} %pad_maximum_fusion.refs_0_), channel_id=1, source_target_pairs={{0,1},{1,0},{2,3},{3,2},{4,5},{5,4},{6,7},{7,6},{8,9},{9,8},{10,11... | collective-permute-start | bytes 2801672 | tf_op jit(solution)/shard_map/ppermute | solution.py:444
  90.0 23.0 %collective-permute-start.19 = (bf16[192,2432]{1,0:T(8,128)(2,1)}, bf16[192,2432]{1,0:T(8,128)(2,1)S(1)}, u32[]{:S(2)}, u32[]{:S(2)}) collective-permute-start(bf16[192,2432]{1,0:T(8,128)(2,1)} %collective-permute-done.14.refs_2_), channel_id=1, source_target_pairs={{0,1},{1,0},{2,3},{3,2},{4,5},{5,4},{6,7},{7,6},{8,9},{9,8},{10,11... | collective-permute-start | bytes 2801672 | tf_op jit(solution)/shard_map/ppermute | solution.py:444
  90.5 22.6 %collective-permute-start.18 = (bf16[192,2432]{1,0:T(8,128)(2,1)}, bf16[192,2432]{1,0:T(8,128)(2,1)}, u32[]{:S(2)}, u32[]{:S(2)}) collective-permute-start(bf16[192,2432]{1,0:T(8,128)(2,1)} %collective-permute-done.13.refs_1_), channel_id=1, source_target_pairs={{0,1},{1,0},{2,3},{3,2},{4,5},{5,4},{6,7},{7,6},{8,9},{9,8},{10,11... | collective-permute-start | bytes 2801672 | tf_op jit(solution)/shard_map/ppermute | solution.py:444
  90.6 22.5 %collective-permute-start.21 = (bf16[96,2432]{1,0:T(8,128)(2,1)S(1)}, bf16[96,2432]{1,0:T(8,128)(2,1)S(1)}, u32[]{:S(2)}, u32[]{:S(2)}) collective-permute-start(bf16[96,2432]{1,0:T(8,128)(2,1)S(1)} %collective-permute-done.16.refs_4_), channel_id=1, source_target_pairs={{0,1},{1,0},{2,3},{3,2},{4,5},{5,4},{6,7},{7,6},{8,9},{9,8},{10,11... | collective-permute-start | bytes 1400840 | tf_op jit(solution)/shard_map/ppermute | solution.py:444
  91.0 22.1 %collective-permute-start.20 = (bf16[96,2432]{1,0:T(8,128)(2,1)}, bf16[96,2432]{1,0:T(8,128)(2,1)}, u32[]{:S(2)}, u32[]{:S(2)}) collective-permute-start(bf16[96,2432]{1,0:T(8,128)(2,1)} %collective-permute-done.15.refs_3_), channel_id=1, source_target_pairs={{0,1},{1,0},{2,3},{3,2},{4,5},{5,4},{6,7},{7,6},{8,9},{9,8},{10,11... | collective-permute-start | bytes 1400840 | tf_op jit(solution)/shard_map/ppermute | solution.py:444
  186.8 22.1 %collective-permute-start.40 = (f32[2,256,768]{2,1,0:T(8,128)}, f32[2,256,768]{2,1,0:T(8,128)S(1)}, u32[]{:S(2)}, u32[]{:S(2)}) collective-permute-start(f32[2,256,768]{2,1,0:T(8,128)} %get-tuple-element.34), channel_id=1, source_target_pairs={{0,1},{1,0},{2,3},{3,2},{4,5},{5,4},{6,7},{7,6},{8,9},{9,8},{10,11... | collective-permute-start | bytes 4718600 | tf_op jit(solution)/shard_map/ppermute | solution.py:444
  187.2 21.6 %collective-permute-start.39 = (bf16[2,256,768]{2,1,0:T(8,128)(2,1)S(1)}, bf16[2,256,768]{2,1,0:T(8,128)(2,1)S(1)}, u32[]{:S(2)}, u32[]{:S(2)}) collective-permute-start(bf16[2,256,768]{2,1,0:T(8,128)(2,1)S(1)} %copy-done.16), channel_id=1, source_target_pairs={{0,1},{1,0},{2,3},{3,2},{4,5},{5,4},{6,7},{7,6},{8,9},{9,8},{10,11... | collective-permute-start | bytes 2359304 | tf_op jit(solution)/shard_map/ppermute | solution.py:444
  (59 other events, 742.4 us)

commit v3 on v2

--- a/solution.py
+++ b/solution.py
@@ -250,38 +250,55 @@
     half_slot = slot // 2
     heads = width // 2
     first, last = chunks
-    parts = [(0, first), (first, first), (2 * first, last), (2 * first + last, last)]
+    size = width
+    parts = list(range(0, 2 * (first + last), size))
+
+    o = heads
+    tail = 2 * first
+    groups = [
+        weight_copies(layouts[0], offsets, pieces, out_weights, sems.at[0], [(0, 0, o, 0), (1, 0, o, o)]),
+        weight_copies(layouts[0], offsets, pieces, in_weights, sems.at[1], [(0, o, first, 0), (1, o, first, first)]),
+        weight_copies(
+            layouts[0], offsets, pieces, back_weights, sems.at[2], [(0, o + first, first, 0), (1, o + first, first, first)]
+        ),
+        weight_copies(
+            layouts[1], offsets, pieces_last, in_weights, sems.at[3], [(0, 0, last, tail), (1, 0, last, tail + last)]
+        ),
+        weight_copies(
+            layouts[1], offsets, pieces_last, back_weights, sems.at[4], [(0, last, last, tail), (1, last, last, tail + last)]
+        ),
+    ]
 
     @pl.when(pl.program_id(0) == 0)
     def _():
-        o = heads
-        copies = weight_copies(layouts[0], offsets, pieces, out_weights, sems.at[0], [(0, 0, o, 0), (1, 0, o, o)])
-        copies += weight_copies(
-            layouts[0], offsets, pieces, in_weights, sems.at[0], [(0, o, first, 0), (1, o, first, first)]
-        )
-        copies += weight_copies(
-            layouts[0], offsets, pieces, back_weights, sems.at[0], [(0, o + first, first, 0), (1, o + first, first, first)]
-        )
-        at = 2 * first
-        copies += weight_copies(
-            layouts[1], offsets, pieces_last, in_weights, sems.at[0], [(0, 0, last, at), (1, 0, last, at + last)]
-        )
-        copies += weight_copies(
-            layouts[1], offsets, pieces_last, back_weights, sems.at[0], [(0, last, last, at), (1, last, last, at + last)]
-        )
-        start_all(copies)
-        wait_all(copies)
-
+        for group in groups:
+            start_all(group)
+
+    def arrived(*which):
+        @pl.when(pl.program_id(0) == 0)
+        def _():
+            for index in which:
+                wait_all(groups[index])
+
+    arrived(0)
     x = jnp.concatenate([x_own_ref[0], x_got_ref[0]], axis=0).astype(F32)
     summed = x + output_bias_ref[0:1] + mm_nt(mixed_ref[0], out_weights[...])
     normal_in, scale_in = normalize(summed)
     normed = normal_in * gain_ref[0:1] + shift_ref[0:1]
     normed_low = normed.astype(BF16)
     total = normed + output_bias_ref[1:2]
-    for at, size in parts:
+    for at in parts:
+        if at == 0:
+            arrived(1)
+        if at < tail < at + size or at == tail:
+            arrived(3)
         pre = mm(normed_low, in_weights[:, at : at + size]) + hidden_bias_ref[:, at : at + size]
         share = 0.5 * (1.0 + lax.erf(pre * 0.7071067811865476))
         slope[:, at : at + size] = share + pre * jnp.exp(-0.5 * pre * pre) * 0.3989422804014327
+        if at == 0:
+            arrived(2)
+        if at < tail < at + size or at == tail:
+            arrived(4)
         total += mm_nt((pre * share).astype(BF16), back_weights[:, at : at + size])
     normal_out, scale_out = normalize(total)
     out = (normal_out * gain_ref[1:2] + shift_ref[1:2]).astype(BF16)
@@ -291,7 +308,7 @@
     grad_total = normalize_back(grad, gain_ref[1:2], normal_out, scale_out)
     grad_low = grad_total.astype(BF16)
     grad_normed = grad_total
-    for at, size in parts:
+    for at in parts:
         grad_pre = (mm(grad_low, back_weights[:, at : at + size]) * slope[:, at : at + size]).astype(BF16)
         grad_normed += mm_nt(grad_pre, in_weights[:, at : at + size])
     grad_hidden = normalize_back(grad_normed, gain_ref[0:1], normal_in, scale_in)
@@ -383,6 +400,7 @@
         grad_hidden_ref,
         up_own_ref,
         up_got_ref,
+        _,
         own_ref,
         got_ref,
         weights,
@@ -391,17 +409,13 @@
     ) = refs[2 * n :]
     slot, width = grad_hidden_ref.shape[1:]
     heads = width // 2
-
-    @pl.when(pl.program_id(0) == 0)
-    def _():
-        copies = load_projections(layout, offsets, pieces, weights, sems.at[0], heads, (6 * heads, 6 * heads + LANES))
-        start_all(copies)
-        up[...] = jnp.zeros_like(up)
-        up[: 2 * RANK] = ups((up_own_ref, up_got_ref), heads)
-        wait_all(copies)
-
+    copies = load_projections(layout, offsets, pieces, weights, sems.at[0], heads, (6 * heads, 6 * heads + LANES))
+    start_all(copies)
+    up[...] = jnp.zeros_like(up)
+    up[: 2 * RANK] = ups((up_own_ref, up_got_ref), heads)
     grads = grads_ref[0]
     small = two_parts(mm_nt(grads, up[...]))
+    wait_all(copies)
     total = grad_hidden_ref[0] + mm_nt(jnp.concatenate([grads, small], axis=1), weights[...])
     own_ref[0] = total[: slot // 2]
     got_ref[0] = total[slot // 2 :]
@@ -423,7 +437,7 @@
     return jax.ShapeDtypeStruct(shape, dtype)
 
 
-def call(kernel, name, scalars, flat, args, outs, scratch, items, flops, moved):
+def call(kernel, name, scalars, flat, args, outs, scratch, items, flops, moved, aliases=None):
     return pl.pallas_call(
         kernel,
         grid_spec=pltpu.PrefetchScalarGridSpec(
@@ -437,6 +451,7 @@
         compiler_params=pltpu.CompilerParams(vmem_limit_bytes=VMEM_LIMIT),
         cost_estimate=pl.CostEstimate(flops=flops, bytes_accessed=moved, transcendentals=0),
         name=name,
+        input_output_aliases=aliases or {},
     )(*scalars, *flat, *[array for array, _ in args])
 
 
@@ -504,8 +519,7 @@
 
     others = (1 - core) * mine
     x_got = swap(lax.dynamic_slice_in_dim(inputs, others, mine, 0))
-    grad_got = swap(lax.dynamic_slice_in_dim(output_gradient, others, mine, 0))
-    bias_got, hidden_bias_got, up_got = swap(query_value_bias), swap(feedforward_input_bias), swap(adapter_up_weight)
+    bias_got, up_got = swap(query_value_bias), swap(adapter_up_weight)
 
     if count == 16:
         offsets = ring_offsets(lax.axis_index("dp"), shard_rows)
@@ -517,24 +531,34 @@
         def to_y(array):
             return move(array, lambda i: i ^ 2)
 
+        def z_move(array, planes):
+            return move(array, lambda i: (i + 4 * planes) % 16)
+
         def along_z(array):
-            return [array] + [move(array, lambda i, d=d: (i + 4 * d) % 16) for d in (1, 2, 3)]
-
-        def far(by_x, by_y):
+            return [array] + [z_move(array, planes) for planes in (1, 2, 3)]
+
+        def far_halves(by_x, by_y):
             half = by_x.shape[0] // 2
-            return [to_y(by_x[:half]), to_x(by_y[half:])]
+            return by_x[:half], by_y[half:]
+
+        def far_moves(low, high):
+            return [to_y(low), to_x(high)]
 
         plane = [shard_last, to_x(shard_last), to_y(shard_last), move(shard_last, lambda i: i ^ 3)]
         line = jnp.concatenate(along_z(shard), axis=0)
+        line, x_got, bias_got, up_got = lax.optimization_barrier((line, x_got, bias_got, up_got))
         plane = jnp.concatenate(plane, axis=0)
         shard_first, plane = lax.optimization_barrier((shard_first, plane, line))[:2]
-        near = [to_x(line), to_y(line)]
-        line_first = jnp.concatenate(along_z(shard_first), axis=0)
-        own = [line, *near, *far(*near)]
-        line_first, plane = lax.optimization_barrier((line_first, plane, own[3], own[4]))[:2]
-        own_last = along_z(plane)
-        near_first = [to_x(line_first), to_y(line_first)]
-        own_first = [line_first, *near_first, *far(*near_first)]
+        by = [to_x(line), to_y(line)]
+        own = [line, *by, *far_moves(*far_halves(*by))]
+        swapped = [swap(piece) for piece in own]
+        ahead, behind = z_move(shard_first, 1), z_move(shard_first, 3)
+        across = z_move(after(shard_first, *by), 2)
+        line_first = jnp.concatenate([shard_first, ahead, across, behind], axis=0)
+        line_first = after(line_first, *own[3:])
+        own_last = along_z(after(plane, line_first, *swapped))
+        by_first = [to_x(line_first), to_y(line_first)]
+        own_first = [line_first, *by_first]
         layout, layout_last = LINE_FIRST, PLANE_FIRST
     else:
         offsets = jnp.zeros((2,), jnp.int32)
@@ -542,8 +566,8 @@
         own, own_first, own_last = (
             [lax.all_gather(s, "dp", axis=0, tiled=True)] for s in (shard, shard_first, shard_last)
         )
-    pieces = (*own, *map(swap, own))
-    pieces_feed = (*own_first, *map(swap, own_first), *own_last, *map(swap, own_last))
+        swapped = [swap(piece) for piece in own]
+    pieces = (*own, *swapped)
 
     first_item = core * mine
     my_lengths = lax.dynamic_slice_in_dim(lengths[:, 0], first_item, mine, 0)
@@ -555,15 +579,6 @@
     both = [query_value_bias[0], blank, query_value_bias[1], bias_got[0], blank, bias_got[1]]
     scale = [ones * 0.125, ones, ones] * 2
     bias = jnp.stack([jnp.concatenate(both), jnp.concatenate(scale)])
-    hidden_bias = jnp.concatenate(
-        [
-            feedforward_input_bias[:first],
-            hidden_bias_got[:first],
-            feedforward_input_bias[first:],
-            hidden_bias_got[first:],
-        ]
-    )[None]
-
     own_block = pl.BlockSpec((1, rows, width), lambda i, *s: (s[-1][0] * mine + i, 0, 0))
     got_block = pl.BlockSpec((1, rows, width), lambda i, *_: (i, 0, 0))
     item = (mine, slot, width)
@@ -602,6 +617,26 @@
         2 * tokens * width * (4 * width + 8 * slot),
         12 * tokens * width,
     )
+    own_first, own_last, grad, hidden_bias_own = lax.optimization_barrier(
+        (own_first, own_last, output_gradient, feedforward_input_bias, mixed)
+    )[:4]
+    if count == 16:
+        ends = far_halves(*own_first[1:])
+        own_first, own_last, ends, grad, hidden_bias_own = lax.optimization_barrier(
+            (own_first, own_last, ends, grad, hidden_bias_own)
+        )
+        own_first += far_moves(*ends)
+    grad_got = swap(lax.dynamic_slice_in_dim(grad, others, mine, 0))
+    hidden_bias_got = swap(hidden_bias_own)
+    hidden_bias = jnp.concatenate(
+        [
+            feedforward_input_bias[:first],
+            hidden_bias_got[:first],
+            feedforward_input_bias[first:],
+            hidden_bias_got[first:],
+        ]
+    )[None]
+    pieces_feed = (*own_first, *map(swap, own_first), *own_last, *map(swap, own_last))
     out, out_send, grad_hidden, grad_mixed = call(
         functools.partial(feed_kernel, (layout, layout_last), (first, last)),
         "feed",
@@ -621,7 +656,7 @@
             pltpu.VMEM((width, 2 * hidden), BF16),
             pltpu.VMEM((width, 2 * hidden), BF16),
             pltpu.VMEM((slot, 2 * hidden), F32),
-            pltpu.SemaphoreType.DMA((1,)),
+            pltpu.SemaphoreType.DMA((5,)),
         ],
         mine,
         4 * tokens * width * (width + 4 * hidden),
@@ -640,30 +675,58 @@
         2 * tokens * width * 20 * slot,
         16 * tokens * width,
     )
-    total, total_send = call(
-        functools.partial(input_grad_kernel, layout),
-        "input_grad",
-        (offsets, core),
-        pieces,
-        [in_item(grads), in_item(grad_hidden), in_whole(adapter_up_weight), in_whole(up_got)],
-        split_out(F32),
-        [
-            pltpu.VMEM((width, 3 * width + 2 * LANES), BF16),
-            pltpu.VMEM((LANES, 3 * width), BF16),
-            pltpu.SemaphoreType.DMA((1,)),
-        ],
-        mine,
-        2 * tokens * width * 3 * width,
-        12 * tokens * width,
-    )
+    def input_grad_of(index, total, grads):
+        at = pl.BlockSpec((1, slot, width), lambda i, *_: (index, 0, 0))
+        at_wide = pl.BlockSpec((1, slot, 3 * width), lambda i, *_: (index, 0, 0))
+        own_at = pl.BlockSpec((1, rows, width), lambda i, *r: (r[-1][0] * mine + index, 0, 0))
+        args = [
+            (grads, at_wide),
+            (grad_hidden, at),
+            in_whole(adapter_up_weight),
+            in_whole(up_got),
+            (total, any_spec()),
+        ]
+        return call(
+            functools.partial(input_grad_kernel, layout),
+            "input_grad",
+            (offsets, core),
+            pieces,
+            args,
+            [(shape_of(inputs.shape, F32), own_at), (shape_of((1, rows, width), F32), got_block)],
+            [
+                pltpu.VMEM((width, 3 * width + 2 * LANES), BF16),
+                pltpu.VMEM((LANES, 3 * width), BF16),
+                pltpu.SemaphoreType.DMA((1,)),
+            ],
+            1,
+            2 * slot * width * 3 * width,
+            12 * slot * width,
+            {2 + len(pieces) + 4: 0},
+        )
+
+    total = jnp.zeros(inputs.shape, F32)
+    sends = []
     adapter = adapter_own + swap(adapter_got)
     if count == 16:
-        for step in (1, 2, 4, 8):
-            adapter = adapter + over_dp(count, adapter, lambda i, step=step: i ^ step)
+        total, send = input_grad_of(0, total, grads)
+        sends.append(swap(send))
+        adapter = after(adapter, total)
+        adapter = (adapter + to_x(adapter)) + (to_y(adapter) + move(adapter, lambda i: i ^ 3))
+        grads_last = after(grads, total)
+        total, send = input_grad_of(1, total, grads_last)
+        sends.append(swap(send))
+        adapter = after(adapter, total)
+        ways = along_z(adapter)
+        adapter = (ways[0] + ways[1]) + (ways[2] + ways[3])
     else:
         adapter = lax.psum(adapter, "dp")
+        for index in range(mine):
+            total, send = input_grad_of(index, total, grads)
+            sends.append(swap(send))
     result = lax.dynamic_update_slice_in_dim(out, swap(out_send), others, 0)
-    input_grad = lax.dynamic_update_slice_in_dim(total, swap(total_send), others, 0)
+    input_grad = total
+    for index, send in enumerate(sends):
+        input_grad = lax.dynamic_update_slice_in_dim(input_grad, send, others + index, 0)
     return result, input_grad, adapter.reshape(2, RANK, heads)
 
 

time: 214 us -> 217 us (1.014)
  waiting for transfers between devices: 64 us -> 45.7 us
  starting transfers between devices: 33.7 us -> 48.2 us
  Pallas kernels: 94.1 us -> 100 us
    ppermute x24 -> x26, waiting for transfers between devices: 59.4 us -> 41.5 us  [over_dp(): return lax.ppermute(array, 'dp', [(i, target(i)) for i in range(count)])]
    ppermute x24 -> x26, starting transfers between devices: 29.3 us -> 44 us  [over_dp(): return lax.ppermute(array, 'dp', [(i, target(i)) for i in range(count)])]
    pallas_call x4 -> x5, Pallas kernels: 94.1 us -> 100 us  [call(): pl.pallas_call(kernel, grid_spec=pltpu.PrefetchScalarGridSpec(num_scalar_...]
    ppermute x22 -> x23, waiting for transfers between devices: 4.63 us -> 4.25 us  [swap(): return lax.ppermute(array, 'tensor', [(0, 1), (1, 0)])]
    ppermute x22 -> x23, starting transfers between devices: 4.41 us -> 4.22 us  [swap(): return lax.ppermute(array, 'tensor', [(0, 1), (1, 0)])]
  transfers between devices with their start and end apart: 46 -> 49, of which waited for: 12 -> 19; matrix products, arithmetic and copies ran while one was open for 5% -> 4% of each run, Pallas kernels for 10% -> 14%
where the time goes in v3:
time: 217 us; the launch traced here: 213 us
  Pallas kernels  100 us (46%)
  starting transfers between devices  48.2 us (22%)
  waiting for transfers between devices  45.7 us (21%)
  local copies, waits for them, and re-layouts  11.7 us (5%)
  other arithmetic  6.05 us (3%)
    pallas_call x5, Pallas kernels, call(): pl.pallas_call(kernel, grid_spec=pltpu.PrefetchScalarGridSpec(num_scalar_...  100 us
    ppermute x26, starting transfers between devices, over_dp(): return lax.ppermute(array, 'dp', [(i, target(i)) for i in range(count)])  44 us
    ppermute x26, waiting for transfers between devices, over_dp(): return lax.ppermute(array, 'dp', [(i, target(i)) for i in range(count)])  41.5 us
  transfers between devices with their start and end apart: 49, of which 19 were waited for; matrix products, arithmetic and copies ran while one was open for 4% of the time, Pallas kernels for 14%

profile of v3, /device:TPU:0, one launch (start us, length us, event | category | flops | bytes accessed | tf_op | source)
XLA Modules:
  0.0 213.2 jit_solution(5856191348484575434)
XLA Ops:
  2.4 3.1 %collective-permute-start.3 = (bf16[48,1280]{1,0:T(8,128)(2,1)S(1)}, bf16[48,1280]{1,0:T(8,128)(2,1)S(1)}, u32[]{:S(2)}, u32[]{:S(2)}) collective-permute-start(bf16[48,1280]{1,0:T(8,128)(2,1)S(1)} %pad_maximum_fusion.4), channel_id=1, source_target_pairs={{0,8},{2,10},{4,12},{6,14},{8,16},{10,18},{12,20},{14,22},{16,24},... | collective-permute-start | bytes 368648 | tf_op jit(solution)/shard_map/ppermute | solution.py:467
  5.5 2.6 %collective-permute-start.4 = (bf16[48,1280]{1,0:T(8,128)(2,1)S(1)}, bf16[48,1280]{1,0:T(8,128)(2,1)S(1)}, u32[]{:S(2)}, u32[]{:S(2)}) collective-permute-start(bf16[48,1280]{1,0:T(8,128)(2,1)S(1)} %pad_maximum_fusion.4), channel_id=1, source_target_pairs={{0,16},{2,18},{4,20},{6,22},{8,24},{10,26},{12,28},{14,30},{16,0},... | collective-permute-start | bytes 368648 | tf_op jit(solution)/shard_map/ppermute | solution.py:467
  13.5 2.7 %collective-permute-done.4 = bf16[48,1280]{1,0:T(8,128)(2,1)S(1)} collective-permute-done((bf16[48,1280]{1,0:T(8,128)(2,1)S(1)}, bf16[48,1280]{1,0:T(8,128)(2,1)S(1)}, u32[]{:S(2)}, u32[]{:S(2)}) %collective-permute-start.4) | collective-permute-done | bytes 122912 | tf_op jit(solution)/shard_map/ppermute | solution.py:467
  22.7 1.8 collective-permute-done.2
  25.3 4.2 %collective-permute-start.13 = (bf16[48,2432]{1,0:T(8,128)(2,1)S(1)}, bf16[48,2432]{1,0:T(8,128)(2,1)S(1)}, u32[]{:S(2)}, u32[]{:S(2)}) collective-permute-start(bf16[48,2432]{1,0:T(8,128)(2,1)S(1)} %pad_maximum_fusion.3), channel_id=1, source_target_pairs={{0,24},{2,26},{4,28},{6,30},{8,0},{10,2},{12,4},{14,6},{16,8},{18,... | collective-permute-start | bytes 700424 | tf_op jit(solution)/shard_map/ppermute | solution.py:467
  29.5 4.1 %collective-permute-done.10.refs_1_ = bf16[192,1280]{1,0:T(8,128)(2,1)S(1)} collective-permute-done((bf16[192,1280]{1,0:T(8,128)(2,1)S(1)}, bf16[192,1280]{1,0:T(8,128)(2,1)S(1)}, u32[]{:S(2)}, u32[]{:S(2)}) %collective-permute-start.10) | collective-permute-done | bytes 491552 | tf_op jit(solution)/shard_map/ppermute | solution.py:467
  34.5 3.3 %collective-permute-start.12 = (bf16[48,2432]{1,0:T(8,128)(2,1)S(1)}, bf16[48,2432]{1,0:T(8,128)(2,1)S(1)}, u32[]{:S(2)}, u32[]{:S(2)}) collective-permute-start(bf16[48,2432]{1,0:T(8,128)(2,1)S(1)} %pad_maximum_fusion.3), channel_id=1, source_target_pairs={{0,16},{2,18},{4,20},{6,22},{8,24},{10,26},{12,28},{14,30},{16,0},... | collective-permute-start | bytes 700424 | tf_op jit(solution)/shard_map/ppermute | solution.py:467
  39.2 2.5 %collective-permute-done.9 = bf16[48,2432]{1,0:T(8,128)(2,1)S(1)} collective-permute-done((bf16[48,2432]{1,0:T(8,128)(2,1)S(1)}, bf16[48,2432]{1,0:T(8,128)(2,1)S(1)}, u32[]{:S(2)}, u32[]{:S(2)}) %collective-permute-start.9) | collective-permute-done | bytes 233504 | tf_op jit(solution)/shard_map/ppermute | solution.py:467
  41.7 9.4 %collective-permute-done.12 = bf16[48,2432]{1,0:T(8,128)(2,1)S(1)} collective-permute-done((bf16[48,2432]{1,0:T(8,128)(2,1)S(1)}, bf16[48,2432]{1,0:T(8,128)(2,1)S(1)}, u32[]{:S(2)}, u32[]{:S(2)}) %collective-permute-start.12) | collective-permute-done | bytes 233504 | tf_op jit(solution)/shard_map/ppermute | solution.py:467
  52.3 2.0 pad_maximum_fusion.refs_0_
  56.1 2.8 %collective-permute-start.24 = (bf16[192,1024]{1,0:T(8,128)(2,1)}, bf16[192,1024]{1,0:T(8,128)(2,1)}, u32[]{:S(2)}, u32[]{:S(2)}) collective-permute-start(bf16[192,1024]{1,0:T(8,128)(2,1)} %pad_maximum_fusion.2.refs_10_), channel_id=1, source_target_pairs={{0,16},{2,18},{4,20},{6,22},{8,24},{10,26},{12,28},{14,30},{16,0},... | collective-permute-start | bytes 1179656 | tf_op jit(solution)/shard_map/ppermute | solution.py:467
  60.5 21.7 %project_attend.1 = (bf16[2,512,2304]{2,1,0:T(8,128)(2,1)}, bf16[2,512,768]{2,1,0:T(8,128)(2,1)}, bf16[2,512,128]{2,1,0:T(8,128)(2,1)}, bf16[2,512,256]{2,1,0:T(8,128)(2,1)}) custom-call(s32[16]{0:T(128)} %fusion.5.offsets, s32[2]{0:T(128)} %get-tuple-element.101.lengths, s32[2]{0:T(128)} %get-tuple-element.102.bounds, s32[1]{0:T(128)} %bitcast.core_ref, ...), custom_call_target="tpu_custom_call" | custom-call | flops 11274289152 | bytes 9437184 | tf_op jit(solution)/shard_map/project_attend/pallas_call | solution.py:441
  82.3 3.8 %collective-permute-done.24.refs_12_ = bf16[192,1024]{1,0:T(8,128)(2,1)} collective-permute-done((bf16[192,1024]{1,0:T(8,128)(2,1)}, bf16[192,1024]{1,0:T(8,128)(2,1)}, u32[]{:S(2)}, u32[]{:S(2)}) %collective-permute-start.24) | collective-permute-done | bytes 393248 | tf_op jit(solution)/shard_map/ppermute | solution.py:467
  93.6 7.8 %collective-permute-done.26.refs_3_ = bf16[96,2432]{1,0:T(8,128)(2,1)S(1)} collective-permute-done((bf16[96,2432]{1,0:T(8,128)(2,1)S(1)}, bf16[96,2432]{1,0:T(8,128)(2,1)S(1)}, u32[]{:S(2)}, u32[]{:S(2)}) %collective-permute-start.26) | collective-permute-done | bytes 466976 | tf_op jit(solution)/shard_map/ppermute | solution.py:467
  101.4 3.5 %collective-permute-done.27.refs_4_ = bf16[96,2432]{1,0:T(8,128)(2,1)S(1)} collective-permute-done((bf16[96,2432]{1,0:T(8,128)(2,1)S(1)}, bf16[96,2432]{1,0:T(8,128)(2,1)S(1)}, u32[]{:S(2)}, u32[]{:S(2)}) %collective-permute-start.27) | collective-permute-done | bytes 466976 | tf_op jit(solution)/shard_map/ppermute | solution.py:467
  109.2 36.6 %feed.1 = (bf16[4,256,768]{2,1,0:T(8,128)(2,1)}, bf16[2,256,768]{2,1,0:T(8,128)(2,1)}, f32[2,512,768]{2,1,0:T(8,128)}, bf16[2,512,768]{2,1,0:T(8,128)(2,1)}) custom-call(s32[16]{0:T(128)} %fusion.5.offsets, s32[1]{0:T(128)} %bitcast.core_ref, bf16[192,2432]{1,0:T(8,128)(2,1)} %pad_maximum_fusion.refs_0_, bf16[192,2432]{1,0:T(8,128)(2,1)} %collective-permute-done.16.refs_1_, ...), custom_call_target="tpu_custom_call" | custom-call | flops 21743271936 | bytes 9437184 | tf_op jit(solution)/shard_map/feed/pallas_call | solution.py:441
  145.7 24.1 %attend_back.1 = (bf16[2,512,2304]{2,1,0:T(8,128)(2,1)}, f32[16,384]{1,0:T(8,128)}, f32[16,384]{1,0:T(8,128)}) custom-call(s32[2]{0:T(128)} %get-tuple-element.101.lengths, s32[2]{0:T(128)} %get-tuple-element.102.bounds, s32[1]{0:T(128)} %bitcast.core_ref, bf16[2,512,2304]{2,1,0:T(8,128)(2,1)} %get-tuple-element.82.refs_0_, ...), custom_call_target="tpu_custom_call" | custom-call | flops 16106127360 | bytes 12582912 | tf_op jit(solution)/shard_map/attend_back/pallas_call | solution.py:441
  169.9 1.9 broadcast_in_dim.15.refs_14_
  171.8 8.9 %input_grad.2 = (f32[4,256,768]{2,1,0:T(8,128)}, f32[1,256,768]{2,1,0:T(8,128)}) custom-call(s32[16]{0:T(128)} %fusion.5.offsets, s32[1]{0:T(128)} %bitcast.core_ref, bf16[192,1280]{1,0:T(8,128)(2,1)} %copy-done, bf16[192,1280]{1,0:T(8,128)(2,1)} %copy-done.1, bf16[192,1280]{1,0:T(8,128)(2,1)} %copy-done.2, ...), custom_call_target="tpu_custom_call", output_to_operand_aliasing={{0}: (16, {})} | custom-call | flops 1811939328 | bytes 4718592 | tf_op jit(solution)/shard_map/input_grad/pallas_call | solution.py:441
  181.4 1.9 collective-permute-done.42
  184.7 2.2 %collective-permute-start.45 = (f32[16,384]{1,0:T(8,128)S(1)}, f32[16,384]{1,0:T(8,128)S(1)}, u32[]{:S(2)}, u32[]{:S(2)}) collective-permute-start(f32[16,384]{1,0:T(8,128)S(1)} %add.58), channel_id=1, source_target_pairs={{0,6},{2,4},{4,2},{6,0},{8,14},{10,12},{12,10},{14,8},{16,22},{18,... | collective-permute-start | bytes 73736 | tf_op jit(solution)/shard_map/ppermute | solution.py:467
  186.9 8.7 %input_grad.3 = (f32[4,256,768]{2,1,0:T(8,128)}, f32[1,256,768]{2,1,0:T(8,128)}) custom-call(s32[16]{0:T(128)} %fusion.5.offsets, s32[1]{0:T(128)} %bitcast.core_ref, bf16[192,1280]{1,0:T(8,128)(2,1)} %copy-done, bf16[192,1280]{1,0:T(8,128)(2,1)} %copy-done.1, bf16[192,1280]{1,0:T(8,128)(2,1)} %copy-done.2, ...), custom_call_target="tpu_custom_call", output_to_operand_aliasing={{0}: (16, {})} | custom-call | flops 1811939328 | bytes 4718592 | tf_op jit(solution)/shard_map/input_grad/pallas_call | solution.py:441
  195.7 8.1 %collective-permute-start.46 = (f32[16,384]{1,0:T(8,128)S(1)}, f32[16,384]{1,0:T(8,128)S(1)}, u32[]{:S(2)}, u32[]{:S(2)}) collective-permute-start(f32[16,384]{1,0:T(8,128)S(1)} %add_add_fusion), channel_id=1, source_target_pairs={{0,8},{2,10},{4,12},{6,14},{8,16},{10,18},{12,20},{14,22},{16,24},... | collective-permute-start | bytes 73736 | tf_op jit(solution)/shard_map/ppermute | solution.py:467
  206.5 2.0 collective-permute-done.47
  (203 shorter events, 42.0 us)
Async XLA Ops:
  19.4 14.2 %collective-permute-start.10 = (bf16[192,1280]{1,0:T(8,128)(2,1)S(1)}, bf16[192,1280]{1,0:T(8,128)(2,1)S(1)}, u32[]{:S(2)}, u32[]{:S(2)}) collective-permute-start(bf16[192,1280]{1,0:T(8,128)(2,1)S(1)} %pad_maximum_fusion.1.refs_0_), channel_id=1, source_target_pairs={{0,2},{2,0},{4,6},{6,4},{8,10},{10,8},{12,14},{14,12},{16,18},{18,... | collective-permute-start | bytes 1474568 | tf_op jit(solution)/shard_map/ppermute | solution.py:467
  20.4 14.1 %collective-permute-start.11 = (bf16[192,1280]{1,0:T(8,128)(2,1)S(1)}, bf16[192,1280]{1,0:T(8,128)(2,1)S(1)}, u32[]{:S(2)}, u32[]{:S(2)}) collective-permute-start(bf16[192,1280]{1,0:T(8,128)(2,1)S(1)} %pad_maximum_fusion.1.refs_0_), channel_id=1, source_target_pairs={{0,4},{2,6},{4,0},{6,2},{8,12},{10,14},{12,8},{14,10},{16,20},{18,... | collective-permute-start | bytes 1474568 | tf_op jit(solution)/shard_map/ppermute | solution.py:467
  25.3 29.0 %collective-permute-start.18 = (bf16[192,1280]{1,0:T(8,128)(2,1)S(1)}, bf16[192,1280]{1,0:T(8,128)(2,1)S(1)}, u32[]{:S(2)}, u32[]{:S(2)}) collective-permute-start(bf16[192,1280]{1,0:T(8,128)(2,1)S(1)} %pad_maximum_fusion.1.refs_0_), channel_id=1, source_target_pairs={{0,1},{1,0},{2,3},{3,2},{4,5},{5,4},{6,7},{7,6},{8,9},{9,8},{10,11... | collective-permute-start | bytes 1474568 | tf_op jit(solution)/shard_map/ppermute | solution.py:459
  25.3 13.3 %collective-permute-start.13 = (bf16[48,2432]{1,0:T(8,128)(2,1)S(1)}, bf16[48,2432]{1,0:T(8,128)(2,1)S(1)}, u32[]{:S(2)}, u32[]{:S(2)}) collective-permute-start(bf16[48,2432]{1,0:T(8,128)(2,1)S(1)} %pad_maximum_fusion.3), channel_id=1, source_target_pairs={{0,24},{2,26},{4,28},{6,30},{8,0},{10,2},{12,4},{14,6},{16,8},{18,... | collective-permute-start | bytes 700424 | tf_op jit(solution)/shard_map/ppermute | solution.py:467
  29.5 12.2 %collective-permute-start.9 = (bf16[48,2432]{1,0:T(8,128)(2,1)S(1)}, bf16[48,2432]{1,0:T(8,128)(2,1)S(1)}, u32[]{:S(2)}, u32[]{:S(2)}) collective-permute-start(bf16[48,2432]{1,0:T(8,128)(2,1)S(1)} %pad_maximum_fusion.3), channel_id=1, source_target_pairs={{0,8},{2,10},{4,12},{6,14},{8,16},{10,18},{12,20},{14,22},{16,24},... | collective-permute-start | bytes 700424 | tf_op jit(solution)/shard_map/ppermute | solution.py:467
  34.5 16.6 %collective-permute-start.12 = (bf16[48,2432]{1,0:T(8,128)(2,1)S(1)}, bf16[48,2432]{1,0:T(8,128)(2,1)S(1)}, u32[]{:S(2)}, u32[]{:S(2)}) collective-permute-start(bf16[48,2432]{1,0:T(8,128)(2,1)S(1)} %pad_maximum_fusion.3), channel_id=1, source_target_pairs={{0,16},{2,18},{4,20},{6,22},{8,24},{10,26},{12,28},{14,30},{16,0},... | collective-permute-start | bytes 700424 | tf_op jit(solution)/shard_map/ppermute | solution.py:467
  37.9 13.9 %collective-permute-start.14 = (bf16[96,1280]{1,0:T(8,128)(2,1)S(1)}, bf16[96,1280]{1,0:T(8,128)(2,1)S(1)}, u32[]{:S(2)}, u32[]{:S(2)}) collective-permute-start(bf16[96,1280]{1,0:T(8,128)(2,1)S(1)} %slice.66), channel_id=1, source_target_pairs={{0,4},{2,6},{4,0},{6,2},{8,12},{10,14},{12,8},{14,10},{16,20},{18,... | collective-permute-start | bytes 737288 | tf_op jit(solution)/shard_map/ppermute | solution.py:467
  38.6 13.7 %collective-permute-start.15 = (bf16[96,1280]{1,0:T(8,128)(2,1)S(1)}, bf16[96,1280]{1,0:T(8,128)(2,1)S(1)}, u32[]{:S(2)}, u32[]{:S(2)}) collective-permute-start(bf16[96,1280]{1,0:T(8,128)(2,1)S(1)} %slice.67), channel_id=1, source_target_pairs={{0,2},{2,0},{4,6},{6,4},{8,10},{10,8},{12,14},{14,12},{16,18},{18,... | collective-permute-start | bytes 737288 | tf_op jit(solution)/shard_map/ppermute | solution.py:467
  41.6 14.4 %collective-permute-start.19 = (bf16[192,1280]{1,0:T(8,128)(2,1)S(1)}, bf16[192,1280]{1,0:T(8,128)(2,1)S(1)}, u32[]{:S(2)}, u32[]{:S(2)}) collective-permute-start(bf16[192,1280]{1,0:T(8,128)(2,1)S(1)} %collective-permute-done.10.refs_1_), channel_id=1, source_target_pairs={{0,1},{1,0},{2,3},{3,2},{4,5},{5,4},{6,7},{7,6},{8,9},{9,8},{10,11... | collective-permute-start | bytes 1474568 | tf_op jit(solution)/shard_map/ppermute | solution.py:459
  54.3 31.8 %collective-permute-start.16 = (bf16[192,2432]{1,0:T(8,128)(2,1)}, bf16[192,2432]{1,0:T(8,128)(2,1)}, u32[]{:S(2)}, u32[]{:S(2)}) collective-permute-start(bf16[192,2432]{1,0:T(8,128)(2,1)} %pad_maximum_fusion.refs_0_), channel_id=1, source_target_pairs={{0,2},{2,0},{4,6},{6,4},{8,10},{10,8},{12,14},{14,12},{16,18},{18,... | collective-permute-start | bytes 2801672 | tf_op jit(solution)/shard_map/ppermute | solution.py:467
  55.5 30.6 %collective-permute-start.17 = (bf16[192,2432]{1,0:T(8,128)(2,1)}, bf16[192,2432]{1,0:T(8,128)(2,1)}, u32[]{:S(2)}, u32[]{:S(2)}) collective-permute-start(bf16[192,2432]{1,0:T(8,128)(2,1)} %pad_maximum_fusion.refs_0_), channel_id=1, source_target_pairs={{0,4},{2,6},{4,0},{6,2},{8,12},{10,14},{12,8},{14,10},{16,20},{18,... | collective-permute-start | bytes 2801672 | tf_op jit(solution)/shard_map/ppermute | solution.py:467
  56.1 26.2 %collective-permute-start.23 = (bf16[192,1024]{1,0:T(8,128)(2,1)}, bf16[192,1024]{1,0:T(8,128)(2,1)}, u32[]{:S(2)}, u32[]{:S(2)}) collective-permute-start(bf16[192,1024]{1,0:T(8,128)(2,1)} %pad_maximum_fusion.2.refs_10_), channel_id=1, source_target_pairs={{0,8},{2,10},{4,12},{6,14},{8,16},{10,18},{12,20},{14,22},{16,24},... | collective-permute-start | bytes 1179656 | tf_op jit(solution)/shard_map/ppermute | solution.py:467
  56.1 30.0 %collective-permute-start.24 = (bf16[192,1024]{1,0:T(8,128)(2,1)}, bf16[192,1024]{1,0:T(8,128)(2,1)}, u32[]{:S(2)}, u32[]{:S(2)}) collective-permute-start(bf16[192,1024]{1,0:T(8,128)(2,1)} %pad_maximum_fusion.2.refs_10_), channel_id=1, source_target_pairs={{0,16},{2,18},{4,20},{6,22},{8,24},{10,26},{12,28},{14,30},{16,0},... | collective-permute-start | bytes 1179656 | tf_op jit(solution)/shard_map/ppermute | solution.py:467
  58.9 27.2 %collective-permute-start.25 = (bf16[192,1024]{1,0:T(8,128)(2,1)}, bf16[192,1024]{1,0:T(8,128)(2,1)}, u32[]{:S(2)}, u32[]{:S(2)}) collective-permute-start(bf16[192,1024]{1,0:T(8,128)(2,1)} %pad_maximum_fusion.2.refs_10_), channel_id=1, source_target_pairs={{0,24},{2,26},{4,28},{6,30},{8,0},{10,2},{12,4},{14,6},{16,8},{18,... | collective-permute-start | bytes 1179656 | tf_op jit(solution)/shard_map/ppermute | solution.py:467
  88.3 13.1 %collective-permute-start.26 = (bf16[96,2432]{1,0:T(8,128)(2,1)S(1)}, bf16[96,2432]{1,0:T(8,128)(2,1)S(1)}, u32[]{:S(2)}, u32[]{:S(2)}) collective-permute-start(bf16[96,2432]{1,0:T(8,128)(2,1)S(1)} %slice.58), channel_id=1, source_target_pairs={{0,4},{2,6},{4,0},{6,2},{8,12},{10,14},{12,8},{14,10},{16,20},{18,... | collective-permute-start | bytes 1400840 | tf_op jit(solution)/shard_map/ppermute | solution.py:467
  91.3 13.6 %collective-permute-start.37 = (bf16[2,256,768]{2,1,0:T(8,128)(2,1)S(1)}, bf16[2,256,768]{2,1,0:T(8,128)(2,1)S(1)}, u32[]{:S(2)}, u32[]{:S(2)}) collective-permute-start(bf16[2,256,768]{2,1,0:T(8,128)(2,1)S(1)} %constant_dynamic-slice_fusion), channel_id=1, source_target_pairs={{0,1},{1,0},{2,3},{3,2},{4,5},{5,4},{6,7},{7,6},{8,9},{9,8},{10,11... | collective-permute-start | bytes 2359304 | tf_op jit(solution)/shard_map/ppermute | solution.py:459
  92.0 13.0 %collective-permute-start.27 = (bf16[96,2432]{1,0:T(8,128)(2,1)S(1)}, bf16[96,2432]{1,0:T(8,128)(2,1)S(1)}, u32[]{:S(2)}, u32[]{:S(2)}) collective-permute-start(bf16[96,2432]{1,0:T(8,128)(2,1)S(1)} %slice.59), channel_id=1, source_target_pairs={{0,2},{2,0},{4,6},{6,4},{8,10},{10,8},{12,14},{14,12},{16,18},{18,... | collective-permute-start | bytes 1400840 | tf_op jit(solution)/shard_map/ppermute | solution.py:467
  92.8 14.6 %collective-permute-start.28 = (bf16[192,2432]{1,0:T(8,128)(2,1)}, bf16[192,2432]{1,0:T(8,128)(2,1)S(1)}, u32[]{:S(2)}, u32[]{:S(2)}) collective-permute-start(bf16[192,2432]{1,0:T(8,128)(2,1)} %pad_maximum_fusion.refs_0_), channel_id=1, source_target_pairs={{0,1},{1,0},{2,3},{3,2},{4,5},{5,4},{6,7},{7,6},{8,9},{9,8},{10,11... | collective-permute-start | bytes 2801672 | tf_op jit(solution)/shard_map/ppermute | solution.py:459
  93.1 14.3 %collective-permute-start.29 = (bf16[192,2432]{1,0:T(8,128)(2,1)}, bf16[192,2432]{1,0:T(8,128)(2,1)S(1)}, u32[]{:S(2)}, u32[]{:S(2)}) collective-permute-start(bf16[192,2432]{1,0:T(8,128)(2,1)} %collective-permute-done.16.refs_1_), channel_id=1, source_target_pairs={{0,1},{1,0},{2,3},{3,2},{4,5},{5,4},{6,7},{7,6},{8,9},{9,8},{10,11... | collective-permute-start | bytes 2801672 | tf_op jit(solution)/shard_map/ppermute | solution.py:459
  180.7 29.4 %collective-permute-start.40 = (f32[1,256,768]{2,1,0:T(8,128)}, f32[1,256,768]{2,1,0:T(8,128)S(1)}, u32[]{:S(2)}, u32[]{:S(2)}) collective-permute-start(f32[1,256,768]{2,1,0:T(8,128)} %get-tuple-element.91), channel_id=1, source_target_pairs={{0,1},{1,0},{2,3},{3,2},{4,5},{5,4},{6,7},{7,6},{8,9},{9,8},{10,11... | collective-permute-start | bytes 2359304 | tf_op jit(solution)/shard_map/ppermute | solution.py:459
  181.3 29.8 %collective-permute-start.39 = (bf16[2,256,768]{2,1,0:T(8,128)(2,1)S(1)}, bf16[2,256,768]{2,1,0:T(8,128)(2,1)S(1)}, u32[]{:S(2)}, u32[]{:S(2)}) collective-permute-start(bf16[2,256,768]{2,1,0:T(8,128)(2,1)S(1)} %copy-done.29), channel_id=1, source_target_pairs={{0,1},{1,0},{2,3},{3,2},{4,5},{5,4},{6,7},{7,6},{8,9},{9,8},{10,11... | collective-permute-start | bytes 2359304 | tf_op jit(solution)/shard_map/ppermute | solution.py:459
  183.3 12.3 %collective-permute-start.43 = (f32[16,384]{1,0:T(8,128)S(1)}, f32[16,384]{1,0:T(8,128)S(1)}, u32[]{:S(2)}, u32[]{:S(2)}) collective-permute-start(f32[16,384]{1,0:T(8,128)S(1)} %add.58), channel_id=1, source_target_pairs={{0,2},{2,0},{4,6},{6,4},{8,10},{10,8},{12,14},{14,12},{16,18},{18,... | collective-permute-start | bytes 73736 | tf_op jit(solution)/shard_map/ppermute | solution.py:467
  184.2 11.5 %collective-permute-start.44 = (f32[16,384]{1,0:T(8,128)S(1)}, f32[16,384]{1,0:T(8,128)S(1)}, u32[]{:S(2)}, u32[]{:S(2)}) collective-permute-start(f32[16,384]{1,0:T(8,128)S(1)} %add.58), channel_id=1, source_target_pairs={{0,4},{2,6},{4,0},{6,2},{8,12},{10,14},{12,8},{14,10},{16,20},{18,... | collective-permute-start | bytes 73736 | tf_op jit(solution)/shard_map/ppermute | solution.py:467
  195.6 16.4 %collective-permute-start.41 = (f32[1,256,768]{2,1,0:T(8,128)}, f32[1,256,768]{2,1,0:T(8,128)S(1)}, u32[]{:S(2)}, u32[]{:S(2)}) collective-permute-start(f32[1,256,768]{2,1,0:T(8,128)} %get-tuple-element.92), channel_id=1, source_target_pairs={{0,1},{1,0},{2,3},{3,2},{4,5},{5,4},{6,7},{7,6},{8,9},{9,8},{10,11... | collective-permute-start | bytes 2359304 | tf_op jit(solution)/shard_map/ppermute | solution.py:459
  (66 other events, 612.3 us)
